TPU v7x, 32 devices: a whole 2x2x4 slice. The times are simulated.
32 devices in a mesh: dp: 2 (over x), tp: 16 (over z, y, core).
Axes of the slice: x: 2, y: 2, z: 4, core: 2. Of those that a mesh axis runs over, the one named last changes fastest.
Arguments:
- token_ids: int32 [2, 2048], P('dp'), parts along dimension 0
- route_idx: int32 [2, 2048, 8], P('dp'), parts along dimension 0
- embed_table: bfloat16 [50304, 2048], P('tp')
- attn_norm: bfloat16 [2048], replicated
- w_query: bfloat16 [2048, 2048], P(None, 'tp')
- w_key: bfloat16 [2048, 2048], P(None, 'tp')
- w_value: bfloat16 [2048, 2048], P(None, 'tp')
- w_out: bfloat16 [2048, 2048], P('tp')
- q_gain: bfloat16 [2048], P('tp')
- k_gain: bfloat16 [2048], P('tp')
- mlp_norm: bfloat16 [2048], replicated
- w_router: bfloat16 [2048, 64], replicated
- w_gate: bfloat16 [64, 2048, 1024], P(None, None, 'tp')
- w_up: bfloat16 [64, 2048, 1024], P(None, None, 'tp')
- w_down: bfloat16 [64, 1024, 2048], P(None, 'tp')
Outputs:
- output: bfloat16 [2, 2048, 2048], P('dp', 'tp'), parts along dimension 0
There are 2 independent parts. A program takes and returns all parts, laid end to end along the dimension named above; an argument that names none is the same for every part.
All inputs are finite; a program needn't handle non-finite values.
Results may differ from a plain program's by a relative error of at most 0.010359.
Values are sent between devices in bfloat16 or wider.
A program may use at most 1 GiB of HBM per device.

v0:
```python
import jax
import jax.numpy as jnp
from jax import lax
from jax.sharding import PartitionSpec as P

HEAD_DIM = 128
NORM_EPS = 1e-5


def rms_scale(act_in, norm_gain):
    act_f32 = act_in.astype(jnp.float32)
    mean_sq = jnp.mean(act_f32 * act_f32, axis=-1, keepdims=True)
    return act_f32 * lax.rsqrt(mean_sq + NORM_EPS) * norm_gain.astype(jnp.float32)


def rope_tables(seq_len):
    half_dim = HEAD_DIM // 2
    inv_freq = 1.0 / (10000.0 ** (jnp.arange(half_dim, dtype=jnp.float32) * (2.0 / HEAD_DIM)))
    angles = jnp.arange(seq_len, dtype=jnp.float32)[:, None] * inv_freq[None, :]
    return jnp.cos(angles), jnp.sin(angles)


def apply_rope(heads_f32, cos_tab, sin_tab):
    half_dim = HEAD_DIM // 2
    first_half = heads_f32[..., :half_dim]
    second_half = heads_f32[..., half_dim:]
    cos_b = cos_tab[:, None, :]
    sin_b = sin_tab[:, None, :]
    rotated = jnp.concatenate([first_half * cos_b - second_half * sin_b, second_half * cos_b + first_half * sin_b], axis=-1)
    return rotated.astype(jnp.bfloat16)


def grouped_ffn(moe_in, flat_choice, gate_vals, w_gate, w_up, w_down):
    tok_count, top_count = flat_choice.shape
    n_exp = w_gate.shape[0]
    model_dim = moe_in.shape[1]
    n_rows = tok_count * top_count
    row_block = max(8, (n_rows // n_exp) // 8 * 8)
    n_blocks = n_rows // row_block + n_exp
    n_slots = n_blocks * row_block
    flat_exp = flat_choice.reshape(n_rows)
    expert_iota = jnp.arange(n_exp, dtype=jnp.int32)
    one_hot = (flat_exp[:, None] == expert_iota[None, :]).astype(jnp.int32)
    counts = jnp.sum(one_hot, axis=0)
    rank_in = jnp.sum((jnp.cumsum(one_hot, axis=0) - one_hot) * one_hot, axis=1)
    padded = (counts + row_block - 1) // row_block * row_block
    pad_end = jnp.cumsum(padded)
    pad_start = pad_end - padded
    slot_of_row = jnp.take(pad_start, flat_exp) + rank_in
    slot_src = jnp.full((n_slots,), n_rows, jnp.int32).at[slot_of_row].set(jnp.arange(n_rows, dtype=jnp.int32))
    slot_tok = slot_src // top_count
    x_slots = jnp.take(moe_in, slot_tok, axis=0, mode="fill", fill_value=0).reshape(n_blocks, row_block, model_dim)
    block_first = jnp.arange(n_blocks, dtype=jnp.int32) * row_block
    block_exp = jnp.minimum(jnp.sum((pad_end[None, :] <= block_first[:, None]).astype(jnp.int32), axis=1), n_exp - 1)
    gate_proj = jnp.einsum("bnd,bdf->bnf", x_slots, jnp.take(w_gate, block_exp, axis=0), preferred_element_type=jnp.float32)
    up_proj = jnp.einsum("bnd,bdf->bnf", x_slots, jnp.take(w_up, block_exp, axis=0), preferred_element_type=jnp.float32)
    hidden_act = (jax.nn.silu(gate_proj) * up_proj).astype(jnp.bfloat16)
    y_slots = jnp.einsum("bnf,bfd->bnd", hidden_act, jnp.take(w_down, block_exp, axis=0), preferred_element_type=jnp.float32).reshape(n_slots, model_dim)
    y_choice = jnp.take(y_slots, slot_of_row, axis=0).reshape(tok_count, top_count, model_dim)
    return jnp.sum(gate_vals[:, :, None] * y_choice, axis=1)


def solution(mesh):
    tp_size = mesh.shape["tp"]
    in_specs = (P("dp", None), P("dp", None, None), P("tp", None), P(None), P(None, "tp"), P(None, "tp"), P(None, "tp"), P("tp", None), P("tp"), P("tp"), P(None), P(None, None), P(None, None, "tp"), P(None, None, "tp"), P(None, "tp", None))

    def device_fn(token_ids, route_idx, embed_table, attn_norm, w_query, w_key, w_value, w_out, q_gain, k_gain, mlp_norm, w_router, w_gate, w_up, w_down):
        batch_loc, seq_len = token_ids.shape
        vocab_loc, model_dim = embed_table.shape
        tp_rank = lax.axis_index("tp")
        local_ids = token_ids - tp_rank * vocab_loc
        in_range = (local_ids >= 0) & (local_ids < vocab_loc)
        looked_up = jnp.take(embed_table, jnp.clip(local_ids, 0, vocab_loc - 1), axis=0)
        embed_part = jnp.where(in_range[..., None], looked_up, jnp.zeros((), jnp.bfloat16))
        x_embed = lax.psum_scatter(embed_part, "tp", scatter_dimension=1, tiled=True)

        x_full = lax.all_gather(x_embed, "tp", axis=1, tiled=True)
        normed = rms_scale(x_full, attn_norm).astype(jnp.bfloat16)
        q_raw = jnp.einsum("bsd,dq->bsq", normed, w_query, preferred_element_type=jnp.float32)
        k_raw = jnp.einsum("bsd,dq->bsq", normed, w_key, preferred_element_type=jnp.float32)
        heads_loc = w_query.shape[1] // HEAD_DIM
        head_shape = (batch_loc, seq_len, heads_loc, HEAD_DIM)
        v_heads = jnp.einsum("bsd,dq->bsq", normed, w_value, preferred_element_type=jnp.float32).astype(jnp.bfloat16).reshape(head_shape)
        sq_sums = jnp.stack([jnp.sum(q_raw * q_raw, axis=-1), jnp.sum(k_raw * k_raw, axis=-1)])
        sq_total = lax.psum(sq_sums, "tp")
        inv_rms = lax.rsqrt(sq_total / (w_query.shape[1] * tp_size) + NORM_EPS)
        cos_tab, sin_tab = rope_tables(seq_len)
        q_heads = apply_rope((q_raw * inv_rms[0][..., None] * q_gain.astype(jnp.float32)).reshape(head_shape), cos_tab, sin_tab)
        k_heads = apply_rope((k_raw * inv_rms[1][..., None] * k_gain.astype(jnp.float32)).reshape(head_shape), cos_tab, sin_tab)
        scores = jnp.einsum("bqhd,bkhd->bhqk", q_heads, k_heads, preferred_element_type=jnp.float32) * (HEAD_DIM ** -0.5)
        positions = jnp.arange(seq_len)
        scores = jnp.where(positions[:, None] >= positions[None, :], scores, -1e30)
        attn_prob = jax.nn.softmax(scores, axis=-1).astype(jnp.bfloat16)
        context = jnp.einsum("bhqk,bkhd->bqhd", attn_prob, v_heads, preferred_element_type=jnp.float32).astype(jnp.bfloat16)
        attn_part = jnp.einsum("bqhd,hde->bqe", context, w_out.reshape(heads_loc, HEAD_DIM, model_dim), preferred_element_type=jnp.float32).astype(jnp.bfloat16)
        attn_out = lax.psum_scatter(attn_part, "tp", scatter_dimension=1, tiled=True)
        hidden = (x_embed.astype(jnp.float32) + attn_out.astype(jnp.float32)).astype(jnp.bfloat16)

        hidden_full = lax.all_gather(hidden, "tp", axis=1, tiled=True)
        moe_in = rms_scale(hidden_full, mlp_norm).astype(jnp.bfloat16).reshape(batch_loc * seq_len, model_dim)
        router_prob = jax.nn.softmax(jnp.dot(moe_in, w_router, preferred_element_type=jnp.float32), axis=-1)
        flat_choice = route_idx.reshape(batch_loc * seq_len, route_idx.shape[-1])
        gate_vals = jnp.take_along_axis(router_prob, flat_choice, axis=1)
        expert_sum = grouped_ffn(moe_in, flat_choice, gate_vals, w_gate, w_up, w_down)
        moe_part = expert_sum.astype(jnp.bfloat16).reshape(batch_loc, seq_len, model_dim)
        moe_out = lax.psum_scatter(moe_part, "tp", scatter_dimension=1, tiled=True)
        return (hidden.astype(jnp.float32) + moe_out.astype(jnp.float32)).astype(jnp.bfloat16)

    return jax.shard_map(device_fn, mesh=mesh, in_specs=in_specs, out_specs=P("dp", "tp", None), check_vma=False)
```

profile of v0, /device:TPU:0, one launch (start us, length us, event | category | flops | bytes accessed | tf_op | source)
XLA Modules:
  0.0 1864.0 jit_solution(13568646006048620278)
XLA Ops:
  6.5 0.8 and_reduce_fusion
  7.4 22.7 %gather_fusion = bf16[2048,2048]{1,0:T(8,128)(2,1)} fusion(bf16[3144,2048]{1,0:T(8,128)(2,1)} %param.19, s32[2048]{0:T(1024)S(1)} %broadcast_clamp_fusion.2), kind=kCustom, calls=%fused_computation.2 | custom fusion | bytes 16785408 | tf_op jit(solution)/shard_map/jit(_take)/gather | solution.py:73
  30.0 7.7 fusion.26
  37.9 106.1 %reduce-scatter.4.cloned.1.call-done = bf16[1,128,2048]{2,1,0:T(8,128)(2,1)} async-done(((bf16[1,2048,2048]{2,1,0:T(8,128)(2,1)}), bf16[1,128,2048]{2,1,0:T(8,128)(2,1)}) %reduce-scatter.4.cloned.1.call-update) | async-done | bytes 524304 | tf_op jit(solution)/shard_map/reduce_scatter | solution.py:75
  144.3 75.8 %all-gather.3.cloned.1.call-done = bf16[1,2048,2048]{2,1,0:T(8,128)(2,1)} async-done(((bf16[1,128,2048]{2,1,0:T(8,128)(2,1)}), bf16[1,2048,2048]{2,1,0:T(8,128)(2,1)}) %all-gather.3.cloned.1.call-update) | async-done | bytes 8388624 | tf_op jit(solution)/shard_map/all_gather | solution.py:77
  220.1 5.1 fusion.13
  225.2 8.6 fusion.25
  233.9 5.9 convolution_convert_fusion
  239.8 6.4 multiply_reduce_fusion.1
  246.2 2.9 multiply_reduce_fusion
  249.2 59.1 %psum.7 = f32[2,1,2048]{2,1,0:T(1,128)S(1)} all-reduce(f32[2,1,2048]{2,1,0:T(1,128)S(1)} %pad_maximum_fusion), channel_id=1, replica_groups=mesh['dp'=2,'tp'=16] {'tp'}, use_global_device_ids=true, to_apply=%region_4.5 | all-reduce | flops 4096 | bytes 32768 | tf_op jit(solution)/shard_map/psum | solution.py:85
  308.6 2.5 fusion.53
  311.1 2.4 fusion.23
  313.5 5.7 copy-done.3
  319.2 4.7 fusion.22
  323.9 13.0 convert_bitcast_fusion.1
  337.0 100.6 %reduce-scatter.6.cloned.1.call-done = bf16[1,128,2048]{2,1,0:T(8,128)(2,1)} async-done(((bf16[1,2048,2048]{2,1,0:T(8,128)(2,1)}), bf16[1,128,2048]{2,1,0:T(8,128)(2,1)}) %reduce-scatter.6.cloned.1.call-update) | async-done | bytes 524304 | tf_op jit(solution)/shard_map/reduce_scatter | solution.py:96
  437.6 2.0 add_convert_fusion.1
  443.0 2.0 copy-done.2
  445.3 5.0 broadcast_add_fusion
  450.3 5.9 copy.34
  456.1 6.3 fusion.29
  463.5 0.7 fusion.78
  465.0 0.7 fusion.80
  465.7 4.6 compare_select_fusion.5
  470.4 13.8 compare_reduce_fusion.56
  484.2 36.2 %select_select_fusion = s32[16384]{0:T(1024)S(1)} fusion(pred[16384]{0:T(1024)(128)(4,1)S(1)} %get-tuple-element.62, pred[16384]{0:T(1024)(128)(4,1)S(1)} %get-tuple-element.60, pred[16384]{0:T(1024)(128)(4,1)S(1)} %get-tuple-element.61, pred[16384]{0:T(1024)(128)(4,1)S(1)} %get-tuple-element.59, pred[16384]{0:T(1024)(128)(4,1)S(1)} %get-tuple-element.58, ...), kind=kLoop, calls=%fused_computation.178 | loop fusion | flops 933888 | bytes 1065188 | tf_op jit(solution)/shard_map/jit(_take)/gather | solution.py:49
  521.0 1.6 reduce_sum.102
  522.8 60.4 %scatter_custom_fusion = s32[32768]{0:T(1024)S(1)} fusion(s32[16384]{0:T(1024)S(1)} %bitcast.166, s32[16384]{0:T(1024)S(1)} %iota.52, s32[]{:T(128)} %constant.173.clone.1), kind=kCustom, calls=%fused_computation.179 | custom fusion | bytes 131076 | tf_op jit(solution)/shard_map/scatter | solution.py:50
  584.6 18.6 gather_fusion.6
  603.2 18.5 gather_fusion.5
  621.7 18.5 gather_fusion.2
  640.9 2.7 compare_and_fusion
  643.6 0.8 broadcast_clamp_fusion
  644.3 5.1 fusion.16
  649.4 8.6 fusion.24
  658.1 6.0 fusion.82
  664.3 130.6 %gather_fusion.4 = f32[16384]{0:T(1024)S(1)} fusion(f32[2048,64]{0,1:T(8,128)S(1)} %fusion.49, s32[16384]{0:T(1024)S(1)} %reshape.701), kind=kCustom, calls=%fused_computation.6 | custom fusion | bytes 262144 | tf_op jit(solution)/shard_map/jit(take_along_axis)/gather | solution.py:103
  794.9 1.6 reshape.704
  796.5 246.2 %gather_fusion.1 = bf16[32768,2048]{1,0:T(8,128)(2,1)} fusion(bf16[2048,2048]{1,0:T(8,128)(2,1)} %fusion.24, s32[32768]{0:T(1024)S(1)} %copy-done.10), kind=kCustom, calls=%fused_computation.3 | custom fusion | bytes 268566528 | tf_op jit(solution)/shard_map/jit(_take)/gather | solution.py:52
  1042.6 1.1 broadcast_select_fusion.7
  1043.7 68.7 %fusion.2 = f32[128,256,64]{1,2,0:T(8,128)} fusion(bf16[128,256,2048]{2,1,0:T(8,128)(2,1)} %bitcast.91, pred[128,256]{1,0:T(8,128)(4,1)S(1)} %copy-done.17, bf16[128,2048,64]{1,2,0:T(8,128)(2,1)} %gather_fusion.6, pred[128]{0:T(512)(128)(4,1)S(1)} %copy-done.16), kind=kOutput, calls=%fused_computation.12 | convolution fusion | flops 8673820672 | bytes 176193664 | tf_op jit(solution)/shard_map/bnd,bdf->bnf/dot_general | solution.py:56
  1112.4 68.1 %multiply_convert_fusion.5 = bf16[128,256,64]{1,2,0:T(8,128)(2,1)} fusion(f32[128,256,64]{1,2,0:T(8,128)} %fusion.2, bf16[128,2048,64]{1,2,0:T(8,128)(2,1)} %gather_fusion.5, pred[128]{0:T(512)(128)(4,1)S(1)} %copy-done.16, bf16[128,256,2048]{2,1,0:T(8,128)(2,1)} %bitcast.91, pred[128,256]{1,0:T(8,128)(4,1)S(1)} %copy-done.17), kind=kOutput, calls=%fused_computation.47.clone.clone.2 | convolution fusion | flops 8686403584 | bytes 180387968 | tf_op jit(solution)/shard_map/bnd,bdf->bnf/dot_general | solution.py:55
  1180.5 103.4 %fusion.8 = f32[128,256,2048]{2,1,0:T(8,128)} fusion(bf16[128,64,2048]{2,1,0:T(8,128)(2,1)} %gather_fusion.2, pred[128]{0:T(512)(128)(4,1)S(1)} %copy-done.16, bf16[128,256,64]{1,2,0:T(8,128)(2,1)} %multiply_convert_fusion.5), kind=kOutput, calls=%fused_computation.18 | convolution fusion | flops 8606711808 | bytes 306184320 | tf_op jit(solution)/shard_map/bnf,bfd->bnd/dot_general | solution.py:58
  1283.9 396.1 %gather_fusion.3 = f32[16384,2048]{1,0:T(8,128)} fusion(f32[32768,2048]{1,0:T(8,128)} %bitcast.94, s32[16384]{0:T(1024)S(1)} %copy-done.13), kind=kCustom, calls=%fused_computation.5 | custom fusion | bytes 268500992 | tf_op jit(solution)/shard_map/jit(_take)/gather | solution.py:59
  1680.0 72.3 %fusion.1 = bf16[2048,2048]{1,0:T(8,128)(2,1)} fusion(f32[16384,2048]{1,0:T(8,128)} %gather_fusion.3, f32[2048,8]{1,0:T(8,128)S(1)} %copy-done.5, pred[2048,8]{1,0:T(8,128)(4,1)S(1)} %copy-done.8), kind=kLoop, calls=%fused_computation.10 | loop fusion | flops 96468992 | bytes 142688256 | tf_op jit(solution)/shard_map/reduce_sum | solution.py:60
  1752.3 102.9 %reduce-scatter.8.cloned.1.call-done = bf16[1,128,2048]{2,1,0:T(8,128)(2,1)} async-done(((bf16[1,2048,2048]{2,1,0:T(8,128)(2,1)}), bf16[1,128,2048]{2,1,0:T(8,128)(2,1)}) %reduce-scatter.8.cloned.1.call-update) | async-done | bytes 524304 | tf_op jit(solution)/shard_map/reduce_scatter | solution.py:106
  1855.2 2.0 add_convert_fusion
  (105 shorter events, 9.3 us)
Async XLA Ops:
  6.5 317.3 %copy-start = (bf16[128,2048]{1,0:T(8,128)(2,1)S(1)}, bf16[128,2048]{1,0:T(8,128)(2,1)}, u32[]{:S(2)}) copy-start(bf16[128,2048]{1,0:T(8,128)(2,1)} %param.24) | copy-start | bytes 1572868
  6.5 137.4 %reduce-scatter.4.cloned.1.call-start = ((), (), s32[]{:S(2)}) async-start(), calls=%async_computation.3 | async-start | bytes 8912896 | tf_op jit(solution)/shard_map/reduce_scatter | solution.py:75
  30.0 114.2 %copy-start.21 = (bf16[128]{0:T(256)(128)(2,1)S(1)}, bf16[128]{0:T(256)(128)(2,1)}, u32[]{:S(2)}) copy-start(bf16[128]{0:T(256)(128)(2,1)} %param.25) | copy-start | bytes 772
  30.0 114.2 %copy-start.22 = (bf16[128]{0:T(256)(128)(2,1)S(1)}, bf16[128]{0:T(256)(128)(2,1)}, u32[]{:S(2)}) copy-start(bf16[128]{0:T(256)(128)(2,1)} %param.26) | copy-start | bytes 772
  30.0 114.2 %copy-start.18 = (bf16[2048]{0:T(1024)(128)(2,1)S(1)}, bf16[2048]{0:T(1024)(128)(2,1)}, u32[]{:S(2)}) copy-start(bf16[2048]{0:T(1024)(128)(2,1)} %param.20) | copy-start | bytes 12292
  37.8 196.1 %copy-start.20 = (bf16[2048,128]{1,0:T(8,128)(2,1)S(1)}, bf16[2048,128]{1,0:T(8,128)(2,1)}, u32[]{:S(2)}) copy-start(bf16[2048,128]{1,0:T(8,128)(2,1)} %param.23) | copy-start | bytes 1572868
  37.8 182.3 %all-gather.3.cloned.1.call-start = ((), (), s32[]{:S(2)}) async-start(), calls=%async_computation.4 | async-start | bytes 8912896 | tf_op jit(solution)/shard_map/all_gather | solution.py:77
  144.0 293.5 %reduce-scatter.6.cloned.1.call-start = ((), (), s32[]{:S(2)}) async-start(), calls=%async_computation.5 | async-start | bytes 8912896 | tf_op jit(solution)/shard_map/reduce_scatter | solution.py:96
  225.2 14.5 copy-start.11
  233.8 12.4 slice-start
  233.8 12.4 copy-start.12
  239.7 6.5 slice-start.1
  313.5 5.7 copy-start.3
  323.9 113.7 %copy-start.7 = (bf16[1,128,2048]{2,1,0:T(8,128)(2,1)S(1)}, bf16[1,128,2048]{2,1,0:T(8,128)(2,1)}, u32[]{:S(2)}) copy-start(bf16[1,128,2048]{2,1,0:T(8,128)(2,1)} %reduce-scatter.4.cloned.1.call-done) | copy-start | bytes 1572868
  323.9 115.7 %copy-start.15 = (s32[1,2048,8]{1,2,0:T(8,128)S(1)}, s32[1,2048,8]{1,2,0:T(8,128)}, u32[]{:S(2)}) copy-start(s32[1,2048,8]{1,2,0:T(8,128)} %param.18) | copy-start | bytes 196612
  323.9 117.6 %copy-start.19 = (bf16[2048]{0:T(1024)(128)(2,1)S(1)}, bf16[2048]{0:T(1024)(128)(2,1)}, u32[]{:S(2)}) copy-start(bf16[2048]{0:T(1024)(128)(2,1)} %param.27) | copy-start | bytes 12292
  336.9 307.4 %all-gather.5.cloned.1.call-start = ((), (), s32[]{:S(2)}) async-start(), calls=%async_computation.6 | async-start | bytes 8912896 | tf_op jit(solution)/shard_map/all_gather | solution.py:99
  439.5 1415.7 %reduce-scatter.8.cloned.1.call-start = ((), (), s32[]{:S(2)}) async-start(), calls=%async_computation.7 | async-start | bytes 8912896 | tf_op jit(solution)/shard_map/reduce_scatter | solution.py:106
  443.0 2.0 copy-start.2
  640.2 17.8 copy-start.14
  664.3 132.1 %copy-start.10 = (s32[32768]{0:T(1024)S(1)}, s32[32768]{0:T(1024)}, u32[]{:S(2)}) copy-start(s32[32768]{0:T(1024)} %broadcast_clamp_fusion) | copy-start | bytes 393220
  796.4 246.2 %copy-start.6 = (f32[2048,8]{1,0:T(8,128)S(1)}, f32[2048,8]{1,0:T(8,128)}, u32[]{:S(2)}) copy-start(f32[2048,8]{1,0:T(8,128)} %reshape.704) | copy-start | bytes 196612
  796.4 246.2 %copy-start.9 = (pred[2048,8]{1,0:T(8,128)(4,1)S(1)}, pred[2048,8]{1,0:T(8,128)(4,1)}, u32[]{:S(2)}) copy-start(pred[2048,8]{1,0:T(8,128)(4,1)} %get-tuple-element.66) | copy-start | bytes 49156
  796.4 247.3 %copy-start.16 = (pred[128]{0:T(512)(128)(4,1)S(1)}, pred[128]{0:T(512)(128)(4,1)}, u32[]{:S(2)}) copy-start(pred[128]{0:T(512)(128)(4,1)} %get-tuple-element.71) | copy-start | bytes 388
  796.4 247.3 %copy-start.17 = (pred[128,256]{1,0:T(8,128)(4,1)S(1)}, pred[128,256]{1,0:T(8,128)(4,1)}, u32[]{:S(2)}) copy-start(pred[128,256]{1,0:T(8,128)(4,1)} %broadcast_in_dim.119) | copy-start | bytes 98308
  1180.5 103.4 %copy-start.13 = (s32[16384]{0:T(1024)S(1)}, s32[16384]{0:T(1024)}, u32[]{:S(2)}) copy-start(s32[16384]{0:T(1024)} %broadcast_clamp_fusion.1) | copy-start | bytes 196612
  1283.9 396.1 %copy-start.5 = (f32[2048,8]{1,0:T(8,128)S(1)}, f32[2048,8]{1,0:T(8,128)}, u32[]{:S(2)}) copy-start(f32[2048,8]{1,0:T(8,128)} %broadcast_select_fusion.7) | copy-start | bytes 196612
  1283.9 396.1 %copy-start.8 = (pred[2048,8]{1,0:T(8,128)(4,1)S(1)}, pred[2048,8]{1,0:T(8,128)(4,1)}, u32[]{:S(2)}) copy-start(pred[2048,8]{1,0:T(8,128)(4,1)} %get-tuple-element.65) | copy-start | bytes 49156
  1680.0 175.2 %copy-start.4 = (bf16[1,128,2048]{2,1,0:T(8,128)(2,1)S(1)}, bf16[1,128,2048]{2,1,0:T(8,128)(2,1)}, u32[]{:S(2)}) copy-start(bf16[1,128,2048]{2,1,0:T(8,128)(2,1)} %add_convert_fusion.1) | copy-start | bytes 1572868
  1680.0 177.2 %copy-start.1 = (bf16[128,2048]{1,0:T(8,128)(2,1)S(1)}, bf16[128,2048]{1,0:T(8,128)(2,1)}, u32[]{:S(2)}) copy-start(bf16[128,2048]{1,0:T(8,128)(2,1)} %param.24) | copy-start | bytes 1572868
Sparse Core Ops, SparseCore 0:
  37.9 106.0 reduce-scatter.3
  146.1 73.9 all-gather.2
  337.0 100.4 reduce-scatter.5
  439.7 73.9 all-gather.4
  1752.4 102.7 reduce-scatter.7
where the time goes:
time: 1880 us; the launch traced here: 1860 us
  local copies, waits for them, and re-layouts  935 us (50%)
  waiting for transfers between devices  386 us (21%)
  matrix products  277 us (15%)
  other arithmetic  193 us (10%)
  blocking collectives  59.1 us (3%)
    gather x1, local copies, waits for them, and re-layouts, grouped_ffn(): jnp.take(y_slots, slot_of_row, axis=0)  396 us
    gather x1, local copies, waits for them, and re-layouts, grouped_ffn(): jnp.take(moe_in, slot_tok, axis=0, mode='fill', fill_value=0)  246 us
    gather x4, local copies, waits for them, and re-layouts, device_fn(): gate_vals = jnp.take_along_axis(router_prob, flat_choice, axis=1)  133 us
    reduce_scatter x1, waiting for transfers between devices, device_fn(): lax.psum_scatter(embed_part, 'tp', scatter_dimension=1, tiled=True)  106 us
    dot_general x1, matrix products, grouped_ffn(): jnp.einsum('bnf,bfd->bnd', hidden_act, jnp.take(w_down, block_exp, axis=0...  103 us
    reduce_scatter x1, waiting for transfers between devices, device_fn(): moe_out = lax.psum_scatter(moe_part, 'tp', scatter_dimension=1, tiled=True)  103 us
    reduce_scatter x1, waiting for transfers between devices, device_fn(): lax.psum_scatter(attn_part, 'tp', scatter_dimension=1, tiled=True)  101 us
    all_gather x1, waiting for transfers between devices, device_fn(): x_full = lax.all_gather(x_embed, 'tp', axis=1, tiled=True)  75.8 us
  transfers between devices with their start and end apart: 5, of which 4 were waited for; matrix products, arithmetic and copies ran while one was open for 11% of the time, Pallas kernels for 0%

commit v1 on v0

v1 whole, which is shorter than its diff:
```python
import jax
import jax.numpy as jnp
from jax import lax
from jax.experimental import pallas as pl
from jax.experimental.pallas import tpu as pltpu
from jax.sharding import PartitionSpec as P

HEAD_DIM = 128
NORM_EPS = 1e-5
N_CHUNKS = 4


def rms_scale(act_in, norm_gain):
    act_f32 = act_in.astype(jnp.float32)
    mean_sq = jnp.mean(act_f32 * act_f32, axis=-1, keepdims=True)
    return act_f32 * lax.rsqrt(mean_sq + NORM_EPS) * norm_gain.astype(jnp.float32)


def rope_tables(seq_len):
    half_dim = HEAD_DIM // 2
    inv_freq = 1.0 / (10000.0 ** (jnp.arange(half_dim, dtype=jnp.float32) * (2.0 / HEAD_DIM)))
    angles = jnp.arange(seq_len, dtype=jnp.float32)[:, None] * inv_freq[None, :]
    return jnp.cos(angles), jnp.sin(angles)


def apply_rope(heads_f32, cos_tab, sin_tab):
    half_dim = HEAD_DIM // 2
    first_half = heads_f32[..., :half_dim]
    second_half = heads_f32[..., half_dim:]
    cos_b = cos_tab[:, None, :]
    sin_b = sin_tab[:, None, :]
    rotated = jnp.concatenate([first_half * cos_b - second_half * sin_b, second_half * cos_b + first_half * sin_b], axis=-1)
    return rotated.astype(jnp.bfloat16)


EXP_PER_STEP = 8
ROW_TILE = 256


def moe_kernel(m_ref, mask_ref, wr_ref, wg_ref, wu_ref, wd_ref, out_ref, acc_ref, gate_ref):
    step = pl.program_id(0)
    n_tok = m_ref.shape[0]
    ff_cols = wg_ref.shape[0]
    n_exp = wr_ref.shape[0]
    exp_ff = ff_cols // EXP_PER_STEP
    nt_dims = (((1,), (1,)), ((), ()))

    @pl.when(step == 0)
    def _():
        logits = lax.dot_general(m_ref[...], wr_ref[...], nt_dims, preferred_element_type=jnp.float32)
        logits = logits - jnp.max(logits, axis=-1, keepdims=True)
        expd = jnp.exp(logits)
        gates = expd / jnp.sum(expd, axis=-1, keepdims=True) * mask_ref[...]
        for grp in range(n_exp // EXP_PER_STEP):
            gate_ref[grp] = gates[:, grp * EXP_PER_STEP:(grp + 1) * EXP_PER_STEP]
        acc_ref[...] = jnp.zeros_like(acc_ref)

    def row_body(i, carry):
        rows = pl.ds(pl.multiple_of(i * ROW_TILE, ROW_TILE), ROW_TILE)
        m_tile = m_ref[rows, :]
        gate_proj = lax.dot_general(m_tile, wg_ref[...], nt_dims, preferred_element_type=jnp.float32)
        up_proj = lax.dot_general(m_tile, wu_ref[...], nt_dims, preferred_element_type=jnp.float32)
        act = (gate_proj / (1.0 + jnp.exp(-gate_proj)) * up_proj).astype(jnp.bfloat16).astype(jnp.float32)
        gates = gate_ref[step, rows, :]
        lane = lax.broadcasted_iota(jnp.int32, (ROW_TILE, 2 * exp_ff), 1)
        pieces = []
        for pair in range(EXP_PER_STEP // 2):
            pieces.append(jnp.where(lane < exp_ff, gates[:, 2 * pair:2 * pair + 1], gates[:, 2 * pair + 1:2 * pair + 2]))
        scaled = act * jnp.concatenate(pieces, axis=1)
        high = scaled.astype(jnp.bfloat16)
        low = (scaled - high.astype(jnp.float32)).astype(jnp.bfloat16)
        down = jnp.dot(high, wd_ref[...], preferred_element_type=jnp.float32) + jnp.dot(low, wd_ref[...], preferred_element_type=jnp.float32)
        acc_ref[rows, :] += down
        return carry

    lax.fori_loop(0, n_tok // ROW_TILE, row_body, 0)

    @pl.when(step == pl.num_programs(0) - 1)
    def _():
        out_ref[...] = acc_ref[...].astype(out_ref.dtype)


def dense_moe(m_rows, mask, wr_t, wg_t, wu_t, w_dn):
    n_tok, model_dim = m_rows.shape
    n_exp = wr_t.shape[0]
    n_ff = wg_t.shape[0]
    step_cols = n_ff // n_exp * EXP_PER_STEP
    flops = 2 * n_tok * model_dim * n_ff * 4
    return pl.pallas_call(
        moe_kernel,
        grid=(n_ff // step_cols,),
        in_specs=[
            pl.BlockSpec((n_tok, model_dim), lambda s: (0, 0)),
            pl.BlockSpec((n_tok, n_exp), lambda s: (0, 0)),
            pl.BlockSpec((n_exp, model_dim), lambda s: (0, 0)),
            pl.BlockSpec((step_cols, model_dim), lambda s: (s, 0)),
            pl.BlockSpec((step_cols, model_dim), lambda s: (s, 0)),
            pl.BlockSpec((step_cols, model_dim), lambda s: (s, 0)),
        ],
        out_specs=pl.BlockSpec((n_tok, model_dim), lambda s: (0, 0)),
        out_shape=jax.ShapeDtypeStruct((n_tok, model_dim), jnp.bfloat16),
        scratch_shapes=[pltpu.VMEM((n_tok, model_dim), jnp.float32), pltpu.VMEM((n_exp // EXP_PER_STEP, n_tok, EXP_PER_STEP), jnp.float32)],
        compiler_params=pltpu.CompilerParams(dimension_semantics=("arbitrary",), vmem_limit_bytes=56 * 1024 * 1024),
        cost_estimate=pl.CostEstimate(flops=flops, bytes_accessed=3 * n_ff * model_dim * 2, transcendentals=n_tok * n_ff),
        name="dense_moe",
    )(m_rows, mask, wr_t, wg_t, wu_t, w_dn)


def solution(mesh):
    tp_size = mesh.shape["tp"]
    in_specs = (P("dp", None), P("dp", None, None), P("tp", None), P(None), P(None, "tp"), P(None, "tp"), P(None, "tp"), P("tp", None), P("tp"), P("tp"), P(None), P(None, None), P(None, None, "tp"), P(None, None, "tp"), P(None, "tp", None))

    def device_fn(token_ids, route_idx, embed_table, attn_norm, w_query, w_key, w_value, w_out, q_gain, k_gain, mlp_norm, w_router, w_gate, w_up, w_down):
        batch_loc, seq_len = token_ids.shape
        vocab_loc, model_dim = embed_table.shape
        tp_rank = lax.axis_index("tp")
        local_ids = token_ids - tp_rank * vocab_loc
        in_range = (local_ids >= 0) & (local_ids < vocab_loc)
        looked_up = jnp.take(embed_table, jnp.clip(local_ids, 0, vocab_loc - 1), axis=0)
        embed_part = jnp.where(in_range[..., None], looked_up, jnp.zeros((), jnp.bfloat16))
        x_embed = lax.psum_scatter(embed_part, "tp", scatter_dimension=1, tiled=True)

        a_loc = rms_scale(x_embed, attn_norm).astype(jnp.bfloat16)
        normed = lax.all_gather(a_loc, "tp", axis=1, tiled=True)
        q_raw = jnp.einsum("bsd,dq->bsq", normed, w_query, preferred_element_type=jnp.float32)
        k_raw = jnp.einsum("bsd,dq->bsq", normed, w_key, preferred_element_type=jnp.float32)
        heads_loc = w_query.shape[1] // HEAD_DIM
        head_shape = (batch_loc, seq_len, heads_loc, HEAD_DIM)
        v_heads = jnp.einsum("bsd,dq->bsq", normed, w_value, preferred_element_type=jnp.float32).astype(jnp.bfloat16).reshape(head_shape)
        sq_sums = jnp.stack([jnp.sum(q_raw * q_raw, axis=-1), jnp.sum(k_raw * k_raw, axis=-1)])
        sq_total = lax.psum(sq_sums, "tp")
        inv_rms = lax.rsqrt(sq_total / (w_query.shape[1] * tp_size) + NORM_EPS)
        cos_tab, sin_tab = rope_tables(seq_len)
        q_heads = apply_rope((q_raw * inv_rms[0][..., None] * q_gain.astype(jnp.float32)).reshape(head_shape), cos_tab, sin_tab)
        k_heads = apply_rope((k_raw * inv_rms[1][..., None] * k_gain.astype(jnp.float32)).reshape(head_shape), cos_tab, sin_tab)
        scores = jnp.einsum("bqhd,bkhd->bhqk", q_heads, k_heads, preferred_element_type=jnp.float32) * (HEAD_DIM ** -0.5)
        positions = jnp.arange(seq_len)
        scores = jnp.where(positions[:, None] >= positions[None, :], scores, -1e30)
        attn_prob = jax.nn.softmax(scores, axis=-1).astype(jnp.bfloat16)
        context = jnp.einsum("bhqk,bkhd->bqhd", attn_prob, v_heads, preferred_element_type=jnp.float32).astype(jnp.bfloat16)
        attn_part = jnp.einsum("bqhd,hde->bqe", context, w_out.reshape(heads_loc, HEAD_DIM, model_dim), preferred_element_type=jnp.float32).astype(jnp.bfloat16)
        attn_out = lax.psum_scatter(attn_part, "tp", scatter_dimension=1, tiled=True)
        hidden = (x_embed.astype(jnp.float32) + attn_out.astype(jnp.float32)).astype(jnp.bfloat16)

        m_loc = rms_scale(hidden, mlp_norm).astype(jnp.bfloat16).reshape(batch_loc * seq_len // tp_size, model_dim)
        n_exp = w_gate.shape[0]
        wg_t = jnp.swapaxes(w_gate, 1, 2).reshape(-1, model_dim)
        wu_t = jnp.swapaxes(w_up, 1, 2).reshape(-1, model_dim)
        w_dn = w_down.reshape(-1, model_dim)
        wr_t = w_router.T
        expert_iota = jnp.arange(n_exp, dtype=jnp.int32)
        chosen = route_idx.reshape(batch_loc * seq_len, -1)
        mask = jnp.any(chosen[:, :, None] == expert_iota[None, None, :], axis=1).astype(jnp.float32)
        rows_loc = m_loc.shape[0]
        rows_chunk = rows_loc // N_CHUNKS
        mask = mask.reshape(tp_size, N_CHUNKS, rows_chunk, n_exp)
        moe_parts = []
        for chunk in range(N_CHUNKS):
            m_chunk = lax.all_gather(m_loc[chunk * rows_chunk:(chunk + 1) * rows_chunk], "tp", axis=0, tiled=True)
            mask_chunk = mask[:, chunk].reshape(tp_size * rows_chunk, n_exp)
            part = dense_moe(m_chunk, mask_chunk, wr_t, wg_t, wu_t, w_dn)
            moe_parts.append(lax.psum_scatter(part, "tp", scatter_dimension=0, tiled=True))
        moe_out = jnp.concatenate(moe_parts, axis=0).reshape(hidden.shape)
        return (hidden.astype(jnp.float32) + moe_out.astype(jnp.float32)).astype(jnp.bfloat16)

    return jax.shard_map(device_fn, mesh=mesh, in_specs=in_specs, out_specs=P("dp", "tp", None), check_vma=False)
```

time: 1880 us -> 862 us (0.46)
  local copies, waits for them, and re-layouts: 935 us -> 27.1 us
  matrix products: 277 us -> 27 us
  Pallas kernels: 0 us -> 191 us
  other arithmetic: 193 us -> 24.7 us
  waiting for transfers between devices: 386 us -> 511 us
    gather x14 -> x0, local copies, waits for them, and re-layouts: 834 us -> none  [the longest x1 396 us: grouped_ffn(): jnp.take(y_slots, slot_of_row, axis=0)]
    dot_general x4 -> x0, matrix products: 246 us -> none  [the longest x1 103 us: grouped_ffn(): jnp.einsum('bnf,bfd->bnd', hidden_act, jnp.take(w_down, block_exp, axis=0...]
    pallas_call x0 -> x4, Pallas kernels: none -> 191 us  [dense_moe(): pl.pallas_call(moe_kernel, grid=(n_ff // step_cols,), in_specs=[pl.BlockS...]
    reduce_scatter x1 -> x4, waiting for transfers between devices: 103 us -> 192 us  [device_fn(): lax.psum_scatter(part, 'tp', scatter_dimension=0, tiled=True)]
    reduce_sum x4 -> x0, other arithmetic: 78.8 us -> none  [the longest x1 72.3 us: grouped_ffn(): return jnp.sum(gate_vals[:, :, None] * y_choice, axis=1)]
    scatter x1 -> x0, local copies, waits for them, and re-layouts: 60.4 us -> none  [grouped_ffn(): jnp.full((n_slots,), n_rows, jnp.int32).at[slot_of_row]]
    gather x8 -> x0, other arithmetic: 56.1 us -> none  [the longest x3 54.7 us: grouped_ffn(): slot_of_row = jnp.take(pad_start, flat_exp) + rank_in]
    all_gather x2 -> x5, waiting for transfers between devices: 75.8 us -> 111 us  [the longest x1 74 us: device_fn(): normed = lax.all_gather(a_loc, 'tp', axis=1, tiled=True)]
  transfers between devices with their start and end apart: 5 -> 11, of which waited for: 4 -> 7; matrix products, arithmetic and copies ran while one was open for 11% -> 0% of each run, Pallas kernels for 0% -> 22%
where the time goes in v1:
time: 862 us; the launch traced here: 855 us
  waiting for transfers between devices  511 us (59%)
  Pallas kernels  191 us (22%)
  blocking collectives  59.1 us (7%)
  local copies, waits for them, and re-layouts  27.1 us (3%)
  matrix products  27 us (3%)
  other arithmetic  24.7 us (3%)
  between operations  13.9 us (2%)
    reduce_scatter x4, waiting for transfers between devices, device_fn(): lax.psum_scatter(part, 'tp', scatter_dimension=0, tiled=True)  192 us
    pallas_call x4, Pallas kernels, dense_moe(): pl.pallas_call(moe_kernel, grid=(n_ff // step_cols,), in_specs=[pl.BlockS...  191 us
    reduce_scatter x1, waiting for transfers between devices, device_fn(): lax.psum_scatter(embed_part, 'tp', scatter_dimension=1, tiled=True)  106 us
    reduce_scatter x1, waiting for transfers between devices, device_fn(): lax.psum_scatter(attn_part, 'tp', scatter_dimension=1, tiled=True)  100 us
    all_gather x1, waiting for transfers between devices, device_fn(): normed = lax.all_gather(a_loc, 'tp', axis=1, tiled=True)  74 us
    psum x1, blocking collectives, device_fn(): sq_total = lax.psum(sq_sums, 'tp')  59.1 us
    all_gather x4, waiting for transfers between devices, device_fn(): lax.all_gather(m_loc[chunk * rows_chunk:(chunk + 1) * rows_chunk], 'tp',...  37.1 us
    gather x1, local copies, waits for them, and re-layouts, device_fn(): jnp.take(embed_table, jnp.clip(local_ids, 0, vocab_loc - 1), axis=0)  22.7 us
  transfers between devices with their start and end apart: 11, of which 7 were waited for; matrix products, arithmetic and copies ran while one was open for 0% of the time, Pallas kernels for 22%

profile of v1, /device:TPU:0, one launch (start us, length us, event | category | flops | bytes accessed | tf_op | source)
XLA Modules:
  0.0 855.2 jit_solution(3203294597661178567)
XLA Ops:
  6.5 0.8 and_reduce_fusion
  7.4 22.7 %gather_fusion = bf16[2048,2048]{1,0:T(8,128)(2,1)} fusion(bf16[3144,2048]{1,0:T(8,128)(2,1)} %param.17, s32[2048]{0:T(1024)S(1)} %broadcast_clamp_fusion), kind=kCustom, calls=%fused_computation | custom fusion | bytes 16785408 | tf_op jit(solution)/shard_map/jit(_take)/gather | solution.py:119
  30.1 7.7 fusion.8
  37.8 0.0 all-gather.10.cloned.1.call-start
  37.9 0.6 copy-done.9
  38.5 105.5 %reduce-scatter.7.cloned.1.call-done = bf16[1,128,2048]{2,1,0:T(8,128)(2,1)} async-done(((bf16[1,2048,2048]{2,1,0:T(8,128)(2,1)}), bf16[1,128,2048]{2,1,0:T(8,128)(2,1)}) %reduce-scatter.7.cloned.1.call-update) | async-done | bytes 524304 | tf_op jit(solution)/shard_map/reduce_scatter | solution.py:121
  144.0 1.2 fusion.16
  145.2 2.0 fusion.18
  147.3 0.0 reduce-scatter.9.cloned.1.call-start
  147.4 74.0 %all-gather.10.cloned.1.call-done = bf16[1,2048,2048]{2,1,0:T(8,128)(2,1)} async-done(((bf16[1,128,2048]{2,1,0:T(8,128)(2,1)}), bf16[1,2048,2048]{2,1,0:T(8,128)(2,1)}) %all-gather.10.cloned.1.call-update) | async-done | bytes 8388624 | tf_op jit(solution)/shard_map/all_gather | solution.py:124
  221.4 6.4 multiply_reduce_fusion
  227.8 2.9 multiply_reduce_fusion.1
  230.8 59.1 %psum.7 = f32[2,1,2048]{2,1,0:T(1,128)S(1)} all-reduce(f32[2,1,2048]{2,1,0:T(1,128)S(1)} %pad_maximum_fusion), channel_id=1, replica_groups=mesh['dp'=2,'tp'=16] {'tp'}, use_global_device_ids=true, to_apply=%region_4.5 | all-reduce | flops 4096 | bytes 32768 | tf_op jit(solution)/shard_map/psum | solution.py:131
  289.9 0.3 multiply_bitcast_fusion
  290.2 2.5 fusion.35
  292.7 2.4 fusion.1
  295.1 4.7 fusion
  299.8 1.0 copy-done.3
  300.8 2.4 fusion.11
  303.2 12.9 %convert_bitcast_fusion = bf16[1,2048,2048]{2,1,0:T(8,128)(2,1)} fusion(bf16[128,2048]{1,0:T(8,128)(2,1)S(1)} %copy-done, bf16[2048,128]{1,0:T(8,128)(2,1)S(1)} %fusion.11, f32[2048,2048]{0,1:T(8,128)} %copy-done.3, f32[2048]{0:T(1024)S(1)} %fusion, f32[2048]{0:T(1024)S(1)} %get-tuple-element.28), kind=kOutput, calls=%fused_computation.15 | convolution fusion | flops 2177105920 | bytes 26230784 | tf_op jit(solution)/shard_map/bqhd,hde->bqe/dot_general | solution.py:141
  316.2 0.0 all-gather.18.cloned.1.call-start
  316.2 0.6 copy-done.10
  316.8 100.0 %reduce-scatter.9.cloned.1.call-done = bf16[1,128,2048]{2,1,0:T(8,128)(2,1)} async-done(((bf16[1,2048,2048]{2,1,0:T(8,128)(2,1)}), bf16[1,128,2048]{2,1,0:T(8,128)(2,1)}) %reduce-scatter.9.cloned.1.call-update) | async-done | bytes 524304 | tf_op jit(solution)/shard_map/reduce_scatter | solution.py:142
  416.8 1.3 fusion.20
  418.1 1.3 fusion.22
  419.4 0.8 fusion.43
  420.2 0.0 all-gather.16.cloned.1.call-start
  420.2 0.5 all-gather.16.cloned.1.call-update
  420.8 0.0 all-gather.14.cloned.1.call-start
  420.8 0.5 all-gather.14.cloned.1.call-update
  421.4 0.0 all-gather.12.cloned.1.call-start
  421.4 0.7 all-gather.12.cloned.1.call-update
  422.1 0.3 reduce-scatter.17.cloned.1.call-start
  422.4 0.7 fusion.10
  423.1 0.3 copy.18
  423.4 1.0 fusion.42
  424.4 37.1 %all-gather.18.cloned.1.call-done = bf16[1,512,2048]{2,1,0:T(8,128)(2,1)} async-done(((bf16[1,32,2048]{2,1,0:T(8,128)(2,1)}), bf16[1,512,2048]{2,1,0:T(8,128)(2,1)}) %all-gather.18.cloned.1.call-update) | async-done | bytes 2097168 | tf_op jit(solution)/shard_map/all_gather | solution.py:159
  461.5 47.8 %dense_moe.7 = bf16[512,2048]{1,0:T(8,128)(2,1)} custom-call(bf16[512,2048]{1,0:T(8,128)(2,1)} %bitcast.103, f32[512,64]{1,0:T(8,128)} %bitcast.77, bf16[64,2048]{1,0:T(8,128)(2,1)} %bitcast.104, bf16[4096,2048]{1,0:T(8,128)(2,1)} %bitcast.88, bf16[4096,2048]{1,0:T(8,128)(2,1)} %bitcast.92, bf16[4096,2048]{1,0:T(8,128)(2,1)} %bitcast.96), custom_call_target="tpu_custom_call" | custom-call | flops 34359738368 | bytes 50331648 | tf_op jit(solution)/shard_map/dense_moe/pallas_call | solution.py:89
  509.4 0.0 reduce-scatter.15.cloned.1.call-start
  509.4 47.9 %dense_moe.6 = bf16[512,2048]{1,0:T(8,128)(2,1)} custom-call(bf16[512,2048]{1,0:T(8,128)(2,1)} %bitcast.102, f32[512,64]{1,0:T(8,128)} %bitcast.76, bf16[64,2048]{1,0:T(8,128)(2,1)} %bitcast.105, bf16[4096,2048]{1,0:T(8,128)(2,1)} %bitcast.89, bf16[4096,2048]{1,0:T(8,128)(2,1)} %bitcast.93, bf16[4096,2048]{1,0:T(8,128)(2,1)} %bitcast.97), custom_call_target="tpu_custom_call" | custom-call | flops 34359738368 | bytes 50331648 | tf_op jit(solution)/shard_map/dense_moe/pallas_call | solution.py:89
  557.3 0.3 reduce-scatter.13.cloned.1.call-start
  557.6 47.9 %dense_moe.5 = bf16[512,2048]{1,0:T(8,128)(2,1)} custom-call(bf16[512,2048]{1,0:T(8,128)(2,1)} %bitcast.101, f32[512,64]{1,0:T(8,128)} %bitcast.75, bf16[64,2048]{1,0:T(8,128)(2,1)} %bitcast.106, bf16[4096,2048]{1,0:T(8,128)(2,1)} %bitcast.90, bf16[4096,2048]{1,0:T(8,128)(2,1)} %bitcast.94, bf16[4096,2048]{1,0:T(8,128)(2,1)} %bitcast.98), custom_call_target="tpu_custom_call" | custom-call | flops 34359738368 | bytes 50331648 | tf_op jit(solution)/shard_map/dense_moe/pallas_call | solution.py:89
  605.6 0.0 reduce-scatter.11.cloned.1.call-start
  605.7 47.9 %dense_moe.4 = bf16[512,2048]{1,0:T(8,128)(2,1)} custom-call(bf16[512,2048]{1,0:T(8,128)(2,1)} %bitcast.100, f32[512,64]{1,0:T(8,128)} %bitcast.74, bf16[64,2048]{1,0:T(8,128)(2,1)} %bitcast.107, bf16[4096,2048]{1,0:T(8,128)(2,1)} %bitcast.91, bf16[4096,2048]{1,0:T(8,128)(2,1)} %bitcast.95, bf16[4096,2048]{1,0:T(8,128)(2,1)} %bitcast.99), custom_call_target="tpu_custom_call" | custom-call | flops 34359738368 | bytes 50331648 | tf_op jit(solution)/shard_map/dense_moe/pallas_call | solution.py:89
  653.6 63.5 %reduce-scatter.15.cloned.1.call-done = bf16[32,2048]{1,0:T(8,128)(2,1)} async-done(((bf16[512,2048]{1,0:T(8,128)(2,1)}), bf16[32,2048]{1,0:T(8,128)(2,1)}) %reduce-scatter.15.cloned.1.call-update) | async-done | bytes 131088 | tf_op jit(solution)/shard_map/reduce_scatter | solution.py:162
  717.1 64.4 %reduce-scatter.13.cloned.1.call-done = bf16[32,2048]{1,0:T(8,128)(2,1)} async-done(((bf16[512,2048]{1,0:T(8,128)(2,1)}), bf16[32,2048]{1,0:T(8,128)(2,1)}) %reduce-scatter.13.cloned.1.call-update) | async-done | bytes 131088 | tf_op jit(solution)/shard_map/reduce_scatter | solution.py:162
  781.5 64.5 %reduce-scatter.11.cloned.1.call-done = bf16[32,2048]{1,0:T(8,128)(2,1)} async-done(((bf16[512,2048]{1,0:T(8,128)(2,1)}), bf16[32,2048]{1,0:T(8,128)(2,1)}) %reduce-scatter.11.cloned.1.call-update) | async-done | bytes 131088 | tf_op jit(solution)/shard_map/reduce_scatter | solution.py:162
  846.1 2.1 fusion.23
  (55 shorter events, 0.4 us)
Async XLA Ops:
  6.5 296.7 %copy-start = (bf16[128,2048]{1,0:T(8,128)(2,1)S(1)}, bf16[128,2048]{1,0:T(8,128)(2,1)}, u32[]{:S(2)}) copy-start(bf16[128,2048]{1,0:T(8,128)(2,1)} %param.22) | copy-start | bytes 1572868
  6.5 137.4 %reduce-scatter.7.cloned.1.call-start = ((), (), s32[]{:S(2)}) async-start(), calls=%async_computation.6 | async-start | bytes 8912896 | tf_op jit(solution)/shard_map/reduce_scatter | solution.py:121
  37.8 0.7 copy-start.9
  37.8 109.5 %copy-start.12 = (bf16[128]{0:T(256)(128)(2,1)S(1)}, bf16[128]{0:T(256)(128)(2,1)}, u32[]{:S(2)}) copy-start(bf16[128]{0:T(256)(128)(2,1)} %param.24) | copy-start | bytes 772
  37.8 109.6 %copy-start.13 = (bf16[128]{0:T(256)(128)(2,1)S(1)}, bf16[128]{0:T(256)(128)(2,1)}, u32[]{:S(2)}) copy-start(bf16[128]{0:T(256)(128)(2,1)} %param.23) | copy-start | bytes 772
  37.8 183.6 %copy-start.6 = (bf16[2048,128]{1,0:T(8,128)(2,1)S(1)}, bf16[2048,128]{1,0:T(8,128)(2,1)}, u32[]{:S(2)}) copy-start(bf16[2048,128]{1,0:T(8,128)(2,1)} %param.20) | copy-start | bytes 1572868
  37.8 183.6 %all-gather.10.cloned.1.call-start = ((), (), s32[]{:S(2)}) async-start(), calls=%async_computation.7 | async-start | bytes 8912896 | tf_op jit(solution)/shard_map/all_gather | solution.py:124
  38.5 189.4 %copy-start.7 = (bf16[2048,128]{1,0:T(8,128)(2,1)S(1)}, bf16[2048,128]{1,0:T(8,128)(2,1)}, u32[]{:S(2)}) copy-start(bf16[2048,128]{1,0:T(8,128)(2,1)} %param.19) | copy-start | bytes 1572868
  147.3 269.5 %reduce-scatter.9.cloned.1.call-start = ((), (), s32[]{:S(2)}) async-start(), calls=%async_computation.8 | async-start | bytes 8912896 | tf_op jit(solution)/shard_map/reduce_scatter | solution.py:142
  221.4 6.5 copy-start.2
  290.2 10.6 %slice-start = ((s8[8388608]{0:T(1024)(128)(4,1)}), s8[4194304]{0:T(1024)(128)(4,1)S(1)}, s32[]{:S(2)}) async-start(s8[8388608]{0:T(1024)(128)(4,1)} %bitcast.71), calls=%async_computation.17 | async-start | bytes 8388608
  292.7 8.2 slice-start.1
  295.1 5.7 copy-start.3
  295.1 5.7 copy-start.11
  316.1 0.7 copy-start.10
  316.1 100.7 %copy-start.4 = (bf16[1,128,2048]{2,1,0:T(8,128)(2,1)S(1)}, bf16[1,128,2048]{2,1,0:T(8,128)(2,1)}, u32[]{:S(2)}) copy-start(bf16[1,128,2048]{2,1,0:T(8,128)(2,1)} %reduce-scatter.7.cloned.1.call-done) | copy-start | bytes 1572868
  316.1 106.2 %copy-start.8 = (s32[1,2048,8]{1,2,0:T(8,128)S(1)}, s32[1,2048,8]{1,2,0:T(8,128)}, u32[]{:S(2)}) copy-start(s32[1,2048,8]{1,2,0:T(8,128)} %param.16) | copy-start | bytes 196612
  316.2 145.4 %all-gather.18.cloned.1.call-start = ((), (), s32[]{:S(2)}) async-start(), calls=%async_computation.16 | async-start | bytes 2228224 | tf_op jit(solution)/shard_map/all_gather | solution.py:159
  420.2 89.2 %all-gather.16.cloned.1.call-start = ((), (), s32[]{:S(2)}) async-start(), calls=%async_computation.15 | async-start | bytes 2228224 | tf_op jit(solution)/shard_map/all_gather | solution.py:159
  420.8 136.8 %all-gather.14.cloned.1.call-start = ((), (), s32[]{:S(2)}) async-start(), calls=%async_computation.14 | async-start | bytes 2228224 | tf_op jit(solution)/shard_map/all_gather | solution.py:159
  421.4 184.3 %all-gather.12.cloned.1.call-start = ((), (), s32[]{:S(2)}) async-start(), calls=%async_computation.13 | async-start | bytes 2228224 | tf_op jit(solution)/shard_map/all_gather | solution.py:159
  422.1 231.5 %reduce-scatter.17.cloned.1.call-start = ((), (), s32[]{:S(2)}) async-start(), calls=%async_computation.12 | async-start | bytes 2228224 | tf_op jit(solution)/shard_map/reduce_scatter | solution.py:162
  509.4 207.8 %reduce-scatter.15.cloned.1.call-start = ((), (), s32[]{:S(2)}) async-start(), calls=%async_computation.11 | async-start | bytes 2228224 | tf_op jit(solution)/shard_map/reduce_scatter | solution.py:162
  557.3 224.2 %reduce-scatter.13.cloned.1.call-start = ((), (), s32[]{:S(2)}) async-start(), calls=%async_computation.10 | async-start | bytes 2228224 | tf_op jit(solution)/shard_map/reduce_scatter | solution.py:162
  605.6 240.5 %reduce-scatter.11.cloned.1.call-start = ((), (), s32[]{:S(2)}) async-start(), calls=%async_computation.9 | async-start | bytes 2228224 | tf_op jit(solution)/shard_map/reduce_scatter | solution.py:162
  605.6 240.4 %copy-start.5 = (bf16[1,128,2048]{2,1,0:T(8,128)(2,1)S(1)}, bf16[1,128,2048]{2,1,0:T(8,128)(2,1)}, u32[]{:S(2)}) copy-start(bf16[1,128,2048]{2,1,0:T(8,128)(2,1)} %reduce-scatter.9.cloned.1.call-done) | copy-start | bytes 1572868
  605.6 242.5 %copy-start.1 = (bf16[128,2048]{1,0:T(8,128)(2,1)S(1)}, bf16[128,2048]{1,0:T(8,128)(2,1)}, u32[]{:S(2)}) copy-start(bf16[128,2048]{1,0:T(8,128)(2,1)} %param.22) | copy-start | bytes 1572868
Sparse Core Ops, SparseCore 0:
  37.9 106.0 reduce-scatter.6
  147.4 73.9 all-gather.9
  316.3 100.4 reduce-scatter.8
  420.3 41.1 all-gather.17
  463.5 40.2 all-gather.15
  505.8 40.2 all-gather.13
  548.3 40.2 all-gather.11
  592.3 60.2 reduce-scatter.16
  656.4 60.7 reduce-scatter.14
  720.7 60.7 reduce-scatter.12
  785.3 60.7 reduce-scatter.10

commit v2 on v1

v2 whole, which is shorter than its diff:
```python
import functools

import jax
import jax.numpy as jnp
from jax import lax
from jax.experimental import pallas as pl
from jax.experimental.pallas import tpu as pltpu
from jax.sharding import PartitionSpec as P

HEAD_DIM = 128
NORM_EPS = 1e-5
N_CHUNKS = 4
EXP_PER_STEP = 8
VMEM_LIMIT = 63 * 1024 * 1024


def rms_scale(act_in, norm_gain):
    act_f32 = act_in.astype(jnp.float32)
    mean_sq = jnp.mean(act_f32 * act_f32, axis=-1, keepdims=True)
    return act_f32 * lax.rsqrt(mean_sq + NORM_EPS) * norm_gain.astype(jnp.float32)


def rope_tables(seq_len):
    half_dim = HEAD_DIM // 2
    inv_freq = 1.0 / (10000.0 ** (jnp.arange(half_dim, dtype=jnp.float32) * (2.0 / HEAD_DIM)))
    angles = jnp.arange(seq_len, dtype=jnp.float32)[:, None] * inv_freq[None, :]
    return jnp.cos(angles), jnp.sin(angles)


def apply_rope(heads_f32, cos_tab, sin_tab):
    half_dim = HEAD_DIM // 2
    first_half = heads_f32[..., :half_dim]
    second_half = heads_f32[..., half_dim:]
    cos_b = cos_tab[:, None, :]
    sin_b = sin_tab[:, None, :]
    rotated = jnp.concatenate([first_half * cos_b - second_half * sin_b, second_half * cos_b + first_half * sin_b], axis=-1)
    return rotated.astype(jnp.bfloat16)


ROW_TILE = 256
N_STAGES = 6
N_Z, N_Y = 4, 2
MESH = pl.DeviceIdType.MESH


class Place:
    def __init__(self):
        self.me = lax.axis_index("tp")
        self.z = self.me // 4
        self.y = self.me % 4 // 2
        self.c = self.me % 2
        self.core_peer = self.me + 1 - 2 * self.c
        self.y_peer = self.me + 2 - 4 * self.y
        self.up = self.me + 4
        self.down = self.me - 4

    def index(self, zz, yy, cc):
        return zz * 4 + yy * 2 + cc


def remote(src, dst, send_sem, recv_sem, device):
    return pltpu.make_async_remote_copy(src_ref=src, dst_ref=dst, send_sem=send_sem, recv_sem=recv_sem, device_id={"tp": device}, device_id_type=MESH)


def entry_barrier(place):
    barrier = pltpu.get_barrier_semaphore()
    for peer in (place.core_peer, place.y_peer):
        pl.semaphore_signal(barrier, inc=1, device_id={"tp": peer}, device_id_type=MESH)

    @pl.when(place.z > 0)
    def _():
        pl.semaphore_signal(barrier, inc=1, device_id={"tp": place.down}, device_id_type=MESH)

    @pl.when(place.z < N_Z - 1)
    def _():
        pl.semaphore_signal(barrier, inc=1, device_id={"tp": place.up}, device_id_type=MESH)

    pl.semaphore_wait(barrier, 2 + (place.z + 3) // 4 + (6 - place.z) // 4)


def by_distance(place, dist, act):
    if dist == 0:
        act(place.z)
        return

    @pl.when(place.z + dist < N_Z)
    def _():
        act(place.z + dist)

    @pl.when(place.z >= dist)
    def _():
        act(place.z - dist)


class Gather:
    SEMS = [(4,), (4,), (4,), (4,), (4,), (8,), (8,)]

    def __init__(self, place, own, shard, sems):
        self.place, self.own, self.shard = place, own, shard
        self.up_send, self.down_send, self.z_recv, self.y_send, self.y_recv, self.c_send, self.c_recv = sems

    def src(self, d, k, mine):
        return self.own(k) if mine else self.shard(d, k)

    def to_up(self, zz, k, mine=False):
        d = self.place.index(zz, self.place.y, self.place.c)
        return remote(self.src(d, k, mine), self.shard(d, k), self.up_send.at[k, zz], self.z_recv.at[k, zz], self.place.up)

    def to_down(self, zz, k, mine=False):
        d = self.place.index(zz, self.place.y, self.place.c)
        return remote(self.src(d, k, mine), self.shard(d, k), self.down_send.at[k, zz], self.z_recv.at[k, zz], self.place.down)

    def to_y(self, zz, k, mine=False, flip=False):
        d = self.place.index(zz, 1 - self.place.y if flip else self.place.y, self.place.c)
        return remote(self.src(d, k, mine), self.shard(d, k), self.y_send.at[k, zz], self.y_recv.at[k, zz], self.place.y_peer)

    def to_core(self, zz, yy, k, mine=False, flip=False):
        d = self.place.index(zz, yy, 1 - self.place.c if flip else self.place.c)
        slot = zz * 2 + yy
        return remote(self.src(d, k, mine), self.shard(d, k), self.c_send.at[k, slot], self.c_recv.at[k, slot], self.place.core_peer)

    def stage(self, number, k):
        place = self.place
        z, y = place.z, place.y
        if number == 0:
            @pl.when(z < N_Z - 1)
            def _():
                self.to_up(z, k, True).start()

            @pl.when(z > 0)
            def _():
                self.to_down(z, k, True).start()

            self.to_y(z, k, True).start()
            self.to_core(z, y, k, True).start()
        elif number < N_Z:
            @pl.when(z >= number)
            def _():
                zz = z - number
                self.to_up(zz, k).wait_recv()

                @pl.when(z < N_Z - 1)
                def _():
                    self.to_up(zz, k).start()

                self.to_y(zz, k).start()
                self.to_core(zz, y, k).start()

            @pl.when(z + number < N_Z)
            def _():
                zz = z + number
                self.to_down(zz, k).wait_recv()

                @pl.when(z > 0)
                def _():
                    self.to_down(zz, k).start()

                self.to_y(zz, k).start()
                self.to_core(zz, y, k).start()
        if 1 <= number <= N_Z:
            def pass_on(zz):
                self.to_y(zz, k, flip=True).wait_recv()
                self.to_core(zz, 1 - y, k).start()

            by_distance(place, number - 1, pass_on)
        if number == N_STAGES - 1:
            for zz in range(N_Z):
                for yy in range(N_Y):
                    self.to_core(zz, yy, k, flip=True).wait_recv()

    def drain(self, k):
        z = self.place.z
        for zz in range(N_Z):
            @pl.when((z >= zz) & (z < N_Z - 1))
            def _():
                self.to_up(zz, k).wait_send()

            @pl.when((z <= zz) & (z > 0))
            def _():
                self.to_down(zz, k).wait_send()

            self.to_y(zz, k).wait_send()
            for yy in range(N_Y):
                self.to_core(zz, yy, k).wait_send()


class Scatter:
    SEMS = [(8,), (8,), (4,), (4,), (4,), (4,), (4,), (4,)]
    BUFS = (8, 4, 4, 4, 4, 4)

    def __init__(self, place, shard, bufs, total, sems):
        self.place, self.shard, self.total = place, shard, total
        self.c_buf, self.y_out, self.y_in, self.z_out, self.from_down, self.from_up = bufs
        self.c_send, self.c_recv, self.y_send, self.y_recv, self.up_send, self.up_recv, self.down_send, self.down_recv = sems

    def to_core(self, zz, yy, k):
        slot = zz * 2 + yy
        d = self.place.index(zz, yy, 1 - self.place.c)
        return remote(self.shard(d, k), self.c_buf.at[k, slot], self.c_send.at[k, slot], self.c_recv.at[k, slot], self.place.core_peer)

    def to_y(self, zz, k):
        return remote(self.y_out.at[k, zz], self.y_in.at[k, zz], self.y_send.at[k, zz], self.y_recv.at[k, zz], self.place.y_peer)

    def to_up(self, zz, k):
        return remote(self.z_out.at[k, zz], self.from_down.at[k, zz], self.up_send.at[k, zz], self.up_recv.at[k, zz], self.place.up)

    def to_down(self, zz, k):
        return remote(self.z_out.at[k, zz], self.from_up.at[k, zz], self.down_send.at[k, zz], self.down_recv.at[k, zz], self.place.down)

    def pair_sum(self, zz, yy, k):
        self.to_core(zz, yy, k).wait_recv()
        mine = self.shard(self.place.index(zz, yy, self.place.c), k)[...].astype(jnp.float32)
        return mine + self.c_buf[k, zz * 2 + yy].astype(jnp.float32)

    def chip_pair_sum(self, zz, k):
        both = self.pair_sum(zz, self.place.y, k)
        self.to_y(zz, k).wait_recv()
        return both + self.y_in[k, zz].astype(jnp.float32)

    def stage(self, number, k):
        place = self.place
        z, y = place.z, place.y
        if number == 0:
            for yy in (1 - y, y):
                for zz in range(N_Z):
                    self.to_core(zz, yy, k).start()
        elif number == 1:
            def send_y(zz):
                self.y_out[k, zz] = self.pair_sum(zz, 1 - y, k).astype(jnp.bfloat16)
                self.to_y(zz, k).start()

            for dist in (3, 2, 1, 0):
                by_distance(place, dist, send_y)
        elif number < N_STAGES - 1:
            dist = N_STAGES - 1 - number

            @pl.when(z + dist < N_Z)
            def _():
                zz = z + dist
                self.total[...] = self.chip_pair_sum(zz, k)

                @pl.when(z > 0)
                def _():
                    self.to_up(zz, k).wait_recv()
                    self.total[...] += self.from_down[k, zz].astype(jnp.float32)

                self.z_out[k, zz] = self.total[...].astype(jnp.bfloat16)
                self.to_up(zz, k).start()

            @pl.when(z >= dist)
            def _():
                zz = z - dist
                self.total[...] = self.chip_pair_sum(zz, k)

                @pl.when(z < N_Z - 1)
                def _():
                    self.to_down(zz, k).wait_recv()
                    self.total[...] += self.from_up[k, zz].astype(jnp.float32)

                self.z_out[k, zz] = self.total[...].astype(jnp.bfloat16)
                self.to_down(zz, k).start()
        else:
            self.total[...] = self.chip_pair_sum(z, k)

            @pl.when(z > 0)
            def _():
                self.to_up(z, k).wait_recv()
                self.total[...] += self.from_down[k, z].astype(jnp.float32)

            @pl.when(z < N_Z - 1)
            def _():
                self.to_down(z, k).wait_recv()
                self.total[...] += self.from_up[k, z].astype(jnp.float32)

    def drain(self, k):
        z = self.place.z
        for zz in range(N_Z):
            for yy in range(N_Y):
                self.to_core(zz, yy, k).wait_send()
            self.to_y(zz, k).wait_send()

            @pl.when(z < zz)
            def _():
                self.to_up(zz, k).wait_send()

            @pl.when(z > zz)
            def _():
                self.to_down(zz, k).wait_send()


def chunk_sems(kind, n_chunks):
    return [pltpu.SemaphoreType.DMA((n_chunks,) + shape) for shape in kind.SEMS]


def chunk_bufs(n_chunks, rows, width):
    return [pltpu.VMEM((n_chunks, slots, rows, width), jnp.bfloat16) for slots in Scatter.BUFS]


def norm_rows(rows_f32, gain_f32):
    mean_sq = jnp.mean(rows_f32 * rows_f32, axis=-1, keepdims=True)
    return (rows_f32 * lax.rsqrt(mean_sq + NORM_EPS) * gain_f32).astype(jnp.bfloat16)


def scatter_kernel(n_chunks, with_residual, *refs):
    n_in = 3 if with_residual else 2
    part, gain = refs[0], refs[1]
    residual = refs[2] if with_residual else None
    sum_ref, norm_ref = refs[n_in:n_in + 2]
    scratch = refs[n_in + 2:]
    total = scratch[0]
    bufs, sems = scratch[1:7], scratch[7:]
    rows = total.shape[0]
    place = Place()
    scat = Scatter(place, lambda d, k: part.at[d, pl.ds(pl.multiple_of(k * rows, rows), rows), :], bufs, total, sems)
    entry_barrier(place)

    def first(k, carry):
        scat.stage(0, k)
        return carry

    def second(k, carry):
        scat.stage(1, k)
        return carry

    def finish(k):
        out_rows = pl.ds(pl.multiple_of(k * rows, rows), rows)
        value = total[...].astype(jnp.bfloat16)
        if residual is not None:
            value = (residual[out_rows, :].astype(jnp.float32) + value.astype(jnp.float32)).astype(jnp.bfloat16)
        sum_ref[out_rows, :] = value
        norm_ref[out_rows, :] = norm_rows(value.astype(jnp.float32), gain[...].astype(jnp.float32))

    def wave(t, carry):
        for number in range(N_STAGES - 1, 1, -1):
            k = t - (number - 2)

            @pl.when((k >= 0) & (k < n_chunks))
            def _():
                scat.stage(number, k)
                if number == N_STAGES - 1:
                    finish(k)
        return carry

    def drain(k, carry):
        scat.drain(k)
        return carry

    lax.fori_loop(0, n_chunks, first, 0)
    lax.fori_loop(0, n_chunks, second, 0)
    lax.fori_loop(0, n_chunks + N_STAGES - 3, wave, 0)
    lax.fori_loop(0, n_chunks, drain, 0)


def scatter_rows(part, gain, residual, collective_id):
    n_dev = N_Z * N_Y * 2
    width = part.shape[-1]
    rows_loc = part.shape[0] // n_dev
    rows = rows_loc // N_CHUNKS
    operands = [part.reshape(n_dev, rows_loc, width), gain.reshape(1, width)]
    if residual is not None:
        operands.append(residual)
    out = jax.ShapeDtypeStruct((rows_loc, width), jnp.bfloat16)
    return pl.pallas_call(
        functools.partial(scatter_kernel, N_CHUNKS, residual is not None),
        in_specs=[pl.BlockSpec(memory_space=pltpu.VMEM)] * len(operands),
        out_specs=[pl.BlockSpec(memory_space=pltpu.VMEM)] * 2,
        out_shape=[out, out],
        scratch_shapes=[pltpu.VMEM((rows, width), jnp.float32)] + chunk_bufs(N_CHUNKS, rows, width) + chunk_sems(Scatter, N_CHUNKS),
        compiler_params=pltpu.CompilerParams(collective_id=collective_id, has_side_effects=True, vmem_limit_bytes=VMEM_LIMIT),
        name="scatter_rows",
    )(*operands)


def gather_kernel(n_chunks, own_ref, out_ref, full, copy_sem, *sems):
    rows = own_ref.shape[0] // n_chunks
    place = Place()
    chunk_rows = lambda k: pl.ds(pl.multiple_of(k * rows, rows), rows)
    gath = Gather(place, lambda k: own_ref.at[chunk_rows(k), :], lambda d, k: full.at[d, chunk_rows(k), :], sems)
    entry_barrier(place)

    def put(k):
        return pltpu.make_async_copy(full.at[:, chunk_rows(k), :], out_ref.at[:, chunk_rows(k), :], copy_sem.at[k])

    def first(k, carry):
        gath.stage(0, k)
        full[place.me, chunk_rows(k), :] = own_ref[chunk_rows(k), :]
        return carry

    def wave(t, carry):
        for number in range(N_STAGES - 1, 0, -1):
            k = t - (number - 1)

            @pl.when((k >= 0) & (k < n_chunks))
            def _():
                gath.stage(number, k)
                if number == N_STAGES - 1:
                    put(k).start()
        return carry

    def drain(k, carry):
        gath.drain(k)
        put(k).wait()
        return carry

    lax.fori_loop(0, n_chunks, first, 0)
    lax.fori_loop(0, n_chunks + N_STAGES - 2, wave, 0)
    lax.fori_loop(0, n_chunks, drain, 0)


def gather_rows(own, collective_id):
    n_dev = N_Z * N_Y * 2
    rows_loc, width = own.shape
    full = pl.pallas_call(
        functools.partial(gather_kernel, N_CHUNKS),
        in_specs=[pl.BlockSpec(memory_space=pltpu.VMEM)],
        out_specs=pl.BlockSpec(memory_space=pl.ANY),
        out_shape=jax.ShapeDtypeStruct((n_dev, rows_loc, width), jnp.bfloat16),
        scratch_shapes=[pltpu.VMEM((n_dev, rows_loc, width), jnp.bfloat16), pltpu.SemaphoreType.DMA((N_CHUNKS,))] + chunk_sems(Gather, N_CHUNKS),
        compiler_params=pltpu.CompilerParams(collective_id=collective_id, has_side_effects=True, vmem_limit_bytes=VMEM_LIMIT),
        name="gather_rows",
    )(own)
    return full.reshape(n_dev * rows_loc, width)


def group_sum_kernel(x_ref, out_ref, slots, send_sem, recv_sem):
    n_dev = slots.shape[0]
    me = lax.axis_index("tp")
    barrier = pltpu.get_barrier_semaphore()
    for off in range(1, n_dev):
        pl.semaphore_signal(barrier, inc=1, device_id={"tp": (me + off) % n_dev}, device_id_type=MESH)
    pl.semaphore_wait(barrier, n_dev - 1)
    for off in range(1, n_dev):
        remote(x_ref, slots.at[me], send_sem.at[off], recv_sem.at[me], (me + off) % n_dev).start()
    slots[me] = x_ref[...]
    for off in range(1, n_dev):
        other = (me + off) % n_dev
        remote(x_ref, slots.at[other], send_sem.at[off], recv_sem.at[other], other).wait_recv()
    out_ref[...] = jnp.sum(slots[...], axis=0)
    for off in range(1, n_dev):
        remote(x_ref, slots.at[me], send_sem.at[off], recv_sem.at[me], (me + off) % n_dev).wait_send()


def group_sum(x, n_dev, collective_id):
    return pl.pallas_call(
        group_sum_kernel,
        in_specs=[pl.BlockSpec(memory_space=pltpu.VMEM)],
        out_specs=pl.BlockSpec(memory_space=pltpu.VMEM),
        out_shape=jax.ShapeDtypeStruct(x.shape, x.dtype),
        scratch_shapes=[pltpu.VMEM((n_dev,) + x.shape, x.dtype), pltpu.SemaphoreType.DMA((n_dev,)), pltpu.SemaphoreType.DMA((n_dev,))],
        compiler_params=pltpu.CompilerParams(collective_id=collective_id, has_side_effects=True),
        name="group_sum",
    )(x)


def moe_kernel(n_chunks, exp_step, own_ref, hid_ref, mask_ref, wr_ref, wg_ref, wu_ref, wd_ref, out_ref, acc_ref, gate_ref, full, part, total, *rest):
    bufs, rest = rest[:6], rest[6:]
    gather_sems, scatter_sems = rest[:len(Gather.SEMS)], rest[len(Gather.SEMS):]
    chunk, step = pl.program_id(0), pl.program_id(1)
    n_steps = pl.num_programs(1)
    rows = own_ref.shape[0] // n_chunks
    n_tok = full.shape[1]
    n_exp = wr_ref.shape[0]
    exp_ff = wg_ref.shape[0] // exp_step
    nt_dims = (((1,), (1,)), ((), ()))
    place = Place()
    loc_rows = lambda k: pl.ds(pl.multiple_of(k * rows, rows), rows)
    block = lambda ref: (lambda d, k: ref.at[k, pl.ds(pl.multiple_of(d * rows, rows), rows), :])
    gath = Gather(place, lambda k: own_ref.at[loc_rows(k), :], block(full), gather_sems)
    scat = Scatter(place, block(part), bufs, total, scatter_sems)

    def finish(k):
        moe_out = total[...].astype(jnp.bfloat16).astype(jnp.float32)
        out_ref[loc_rows(k), :] = (hid_ref[loc_rows(k), :].astype(jnp.float32) + moe_out).astype(jnp.bfloat16)

    @pl.when((chunk == 0) & (step == 0))
    def _():
        entry_barrier(place)
        for k in range(n_chunks):
            full[k, pl.ds(pl.multiple_of(place.me * rows, rows), rows), :] = own_ref[k * rows:(k + 1) * rows, :]
        for number in range(N_STAGES):
            gath.stage(number, 0)

    for number in range(N_STAGES):
        @pl.when((step == number) & (chunk + 1 < n_chunks))
        def _():
            gath.stage(number, chunk + 1)

        @pl.when((step == number) & (chunk > 0))
        def _():
            scat.stage(number, chunk - 1)
            if number == N_STAGES - 1:
                finish(chunk - 1)

    @pl.when(step == 0)
    def _():
        logits = lax.dot_general(full[chunk], wr_ref[...], nt_dims, preferred_element_type=jnp.float32)
        logits = logits - jnp.max(logits, axis=-1, keepdims=True)
        expd = jnp.exp(logits)
        gates = expd / jnp.sum(expd, axis=-1, keepdims=True) * mask_ref[0]
        for grp in range(n_exp // exp_step):
            gate_ref[grp] = gates[:, grp * exp_step:(grp + 1) * exp_step]
        acc_ref[...] = jnp.zeros_like(acc_ref)

    def row_body(i, carry):
        tile = pl.ds(pl.multiple_of(i * ROW_TILE, ROW_TILE), ROW_TILE)
        m_tile = full[chunk, tile, :]
        gate_proj = lax.dot_general(m_tile, wg_ref[...], nt_dims, preferred_element_type=jnp.float32)
        up_proj = lax.dot_general(m_tile, wu_ref[...], nt_dims, preferred_element_type=jnp.float32)
        act = (gate_proj / (1.0 + jnp.exp(-gate_proj)) * up_proj).astype(jnp.bfloat16).astype(jnp.float32)
        gates = gate_ref[step, tile, :]
        lane = lax.broadcasted_iota(jnp.int32, (ROW_TILE, 2 * exp_ff), 1)
        pieces = []
        for pair in range(exp_step // 2):
            pieces.append(jnp.where(lane < exp_ff, gates[:, 2 * pair:2 * pair + 1], gates[:, 2 * pair + 1:2 * pair + 2]))
        scaled = act * jnp.concatenate(pieces, axis=1)
        high = scaled.astype(jnp.bfloat16)
        low = (scaled - high.astype(jnp.float32)).astype(jnp.bfloat16)
        down = jnp.dot(high, wd_ref[...], preferred_element_type=jnp.float32) + jnp.dot(low, wd_ref[...], preferred_element_type=jnp.float32)
        acc_ref[tile, :] += down
        return carry

    lax.fori_loop(0, n_tok // ROW_TILE, row_body, 0)

    @pl.when(step == n_steps - 1)
    def _():
        part[chunk] = acc_ref[...].astype(jnp.bfloat16)

    @pl.when((step == n_steps - 1) & (chunk == n_chunks - 1))
    def _():
        for number in range(N_STAGES):
            scat.stage(number, n_chunks - 1)
        finish(n_chunks - 1)

        def drain(k, carry):
            gath.drain(k)
            scat.drain(k)
            return carry

        lax.fori_loop(0, n_chunks, drain, 0)


def moe_layer(own, hidden, mask, wr_t, wg_t, wu_t, w_dn, collective_id):
    rows_loc, width = own.shape
    n_chunks, n_tok, n_exp = mask.shape
    n_ff = wg_t.shape[0]
    step_cols = n_ff // n_exp * EXP_PER_STEP
    rows = rows_loc // n_chunks
    const = lambda k, s: (0, 0)
    return pl.pallas_call(
        functools.partial(moe_kernel, n_chunks, EXP_PER_STEP),
        grid=(n_chunks, n_ff // step_cols),
        in_specs=[
            pl.BlockSpec((rows_loc, width), const),
            pl.BlockSpec((rows_loc, width), const),
            pl.BlockSpec((1, n_tok, n_exp), lambda k, s: (k, 0, 0)),
            pl.BlockSpec((n_exp, width), const),
            pl.BlockSpec((step_cols, width), lambda k, s: (s, 0)),
            pl.BlockSpec((step_cols, width), lambda k, s: (s, 0)),
            pl.BlockSpec((step_cols, width), lambda k, s: (s, 0)),
        ],
        out_specs=pl.BlockSpec((rows_loc, width), const),
        out_shape=jax.ShapeDtypeStruct((rows_loc, width), jnp.bfloat16),
        scratch_shapes=[
            pltpu.VMEM((n_tok, width), jnp.float32),
            pltpu.VMEM((n_exp // EXP_PER_STEP, n_tok, EXP_PER_STEP), jnp.float32),
            pltpu.VMEM((n_chunks, n_tok, width), jnp.bfloat16),
            pltpu.VMEM((n_chunks, n_tok, width), jnp.bfloat16),
            pltpu.VMEM((rows, width), jnp.float32),
        ] + chunk_bufs(n_chunks, rows, width) + chunk_sems(Gather, n_chunks) + chunk_sems(Scatter, n_chunks),
        compiler_params=pltpu.CompilerParams(dimension_semantics=("arbitrary", "arbitrary"), collective_id=collective_id, has_side_effects=True, vmem_limit_bytes=VMEM_LIMIT),
        name="moe_layer",
    )(own, hidden, mask, wr_t, wg_t, wu_t, w_dn)


def solution(mesh):
    tp_size = mesh.shape["tp"]
    in_specs = (P("dp", None), P("dp", None, None), P("tp", None), P(None), P(None, "tp"), P(None, "tp"), P(None, "tp"), P("tp", None), P("tp"), P("tp"), P(None), P(None, None), P(None, None, "tp"), P(None, None, "tp"), P(None, "tp", None))

    def device_fn(token_ids, route_idx, embed_table, attn_norm, w_query, w_key, w_value, w_out, q_gain, k_gain, mlp_norm, w_router, w_gate, w_up, w_down):
        batch_loc, seq_len = token_ids.shape
        vocab_loc, model_dim = embed_table.shape
        tp_rank = lax.axis_index("tp")
        local_ids = token_ids - tp_rank * vocab_loc
        in_range = (local_ids >= 0) & (local_ids < vocab_loc)
        looked_up = jnp.take(embed_table, jnp.clip(local_ids, 0, vocab_loc - 1), axis=0)
        embed_part = jnp.where(in_range[..., None], looked_up, jnp.zeros((), jnp.bfloat16))
        x_loc, a_loc = scatter_rows(embed_part.reshape(-1, model_dim), attn_norm, None, 0)
        normed = gather_rows(a_loc, 1).reshape(batch_loc, seq_len, model_dim)
        q_raw = jnp.einsum("bsd,dq->bsq", normed, w_query, preferred_element_type=jnp.float32)
        k_raw = jnp.einsum("bsd,dq->bsq", normed, w_key, preferred_element_type=jnp.float32)
        heads_loc = w_query.shape[1] // HEAD_DIM
        head_shape = (batch_loc, seq_len, heads_loc, HEAD_DIM)
        v_heads = jnp.einsum("bsd,dq->bsq", normed, w_value, preferred_element_type=jnp.float32).astype(jnp.bfloat16).reshape(head_shape)
        sq_sums = jnp.stack([jnp.sum(q_raw * q_raw, axis=-1), jnp.sum(k_raw * k_raw, axis=-1)])
        sq_total = group_sum(sq_sums.reshape(2, -1), tp_size, 2).reshape(sq_sums.shape)
        inv_rms = lax.rsqrt(sq_total / (w_query.shape[1] * tp_size) + NORM_EPS)
        cos_tab, sin_tab = rope_tables(seq_len)
        q_heads = apply_rope((q_raw * inv_rms[0][..., None] * q_gain.astype(jnp.float32)).reshape(head_shape), cos_tab, sin_tab)
        k_heads = apply_rope((k_raw * inv_rms[1][..., None] * k_gain.astype(jnp.float32)).reshape(head_shape), cos_tab, sin_tab)
        scores = jnp.einsum("bqhd,bkhd->bhqk", q_heads, k_heads, preferred_element_type=jnp.float32) * (HEAD_DIM ** -0.5)
        positions = jnp.arange(seq_len)
        scores = jnp.where(positions[:, None] >= positions[None, :], scores, -1e30)
        attn_prob = jax.nn.softmax(scores, axis=-1).astype(jnp.bfloat16)
        context = jnp.einsum("bhqk,bkhd->bqhd", attn_prob, v_heads, preferred_element_type=jnp.float32).astype(jnp.bfloat16)
        attn_part = jnp.einsum("bqhd,hde->bqe", context, w_out.reshape(heads_loc, HEAD_DIM, model_dim), preferred_element_type=jnp.float32).astype(jnp.bfloat16)
        h_loc, m_loc = scatter_rows(attn_part.reshape(-1, model_dim), mlp_norm, x_loc, 3)
        n_exp = w_gate.shape[0]
        wg_t = jnp.swapaxes(w_gate, 1, 2).reshape(-1, model_dim)
        wu_t = jnp.swapaxes(w_up, 1, 2).reshape(-1, model_dim)
        w_dn = w_down.reshape(-1, model_dim)
        wr_t = w_router.T
        expert_iota = jnp.arange(n_exp, dtype=jnp.int32)
        chosen = route_idx.reshape(batch_loc * seq_len, -1)
        mask = jnp.any(chosen[:, :, None] == expert_iota[None, None, :], axis=1).astype(jnp.float32)
        rows_chunk = m_loc.shape[0] // N_CHUNKS
        mask = mask.reshape(tp_size, N_CHUNKS, rows_chunk, n_exp).swapaxes(0, 1).reshape(N_CHUNKS, tp_size * rows_chunk, n_exp)
        out_loc = moe_layer(m_loc, h_loc, mask, wr_t, wg_t, wu_t, w_dn, 4)
        return out_loc.reshape(batch_loc, -1, model_dim)

    return jax.shard_map(device_fn, mesh=mesh, in_specs=in_specs, out_specs=P("dp", "tp", None), check_vma=False)
```

time: 862 us -> 521 us (0.60)
  waiting for transfers between devices: 511 us -> 0 us
  Pallas kernels: 191 us -> 438 us
  blocking collectives: 59.1 us -> 0 us
  between operations: 13.9 us -> 0.26 us
    reduce_scatter x6 -> x0, waiting for transfers between devices: 398 us -> none  [the longest x4 192 us: device_fn(): lax.psum_scatter(part, 'tp', scatter_dimension=0, tiled=True)]
    pallas_call x4 -> x5, Pallas kernels: 191 us -> 438 us  [the longest x1 244 us: moe_layer(): pl.pallas_call(functools.partial(moe_kernel, n_chunks, EXP_PER_STEP), gri...]
    all_gather x5 -> x0, waiting for transfers between devices: 111 us -> none  [the longest x1 74 us: device_fn(): normed = lax.all_gather(a_loc, 'tp', axis=1, tiled=True)]
    psum x1 -> x0, blocking collectives: 59.1 us -> none  [device_fn(): sq_total = lax.psum(sq_sums, 'tp')]
  transfers between devices with their start and end apart: 11 -> 0, of which waited for: 7 -> 0; matrix products, arithmetic and copies ran while one was open for 0% -> 0% of each run, Pallas kernels for 22% -> 0%
where the time goes in v2:
time: 521 us; the launch traced here: 520 us
  Pallas kernels  438 us (84%)
  local copies, waits for them, and re-layouts  32.9 us (6%)
  matrix products  31.5 us (6%)
  other arithmetic  17.7 us (3%)
    pallas_call x1, Pallas kernels, moe_layer(): pl.pallas_call(functools.partial(moe_kernel, n_chunks, EXP_PER_STEP), gri...  244 us
    pallas_call x2, Pallas kernels, scatter_rows(): pl.pallas_call(functools.partial(scatter_kernel, N_CHUNKS, residual is no...  131 us
    pallas_call x1, Pallas kernels, gather_rows(): pl.pallas_call(functools.partial(gather_kernel, N_CHUNKS), in_specs=[pl.B...  52.8 us
    gather x1, local copies, waits for them, and re-layouts, device_fn(): jnp.take(embed_table, jnp.clip(local_ids, 0, vocab_loc - 1), axis=0)  22.6 us
    dot_general x1, matrix products, device_fn(): jnp.einsum('bqhd,hde->bqe', context, w_out.reshape(heads_loc, HEAD_DIM, m...  12.9 us

profile of v2, /device:TPU:0, one launch (start us, length us, event | category | flops | bytes accessed | tf_op | source)
XLA Modules:
  0.0 520.2 jit_solution(4313511402857681512)
XLA Ops:
  0.0 0.0 copy-start
  0.0 0.8 and_reduce_fusion
  0.9 22.6 %gather_fusion = bf16[2048,2048]{1,0:T(8,128)(2,1)} fusion(bf16[3144,2048]{1,0:T(8,128)(2,1)} %param.17, s32[2048]{0:T(1024)S(1)} %broadcast_clamp_fusion), kind=kCustom, calls=%fused_computation | custom fusion | bytes 16785408 | tf_op jit(solution)/shard_map/jit(_take)/gather | solution.py:585
  23.5 0.0 copy-start.4
  23.5 7.4 %select_select_fusion.refs_0_ = bf16[16,128,2048]{2,1,0:T(8,128)(2,1)} fusion(bf16[16,128,2048]{2,1,0:T(8,128)(2,1)} %bitcast.59, pred[16,128]{1,0:T(8,128)(4,1)S(1)} %bitcast.74, pred[16,128]{1,0:T(8,128)(4,1)S(1)} %bitcast.75), kind=kLoop, calls=%fused_computation.7 | loop fusion | flops 8388608 | bytes 16781312 | tf_op jit(solution)/shard_map/jit(_where)/select_n | solution.py:586
  30.9 0.0 copy-done.4
  30.9 0.6 reshape.239.refs_1_
  31.5 65.5 %scatter_rows.2 = (bf16[128,2048]{1,0:T(8,128)(2,1)}, bf16[128,2048]{1,0:T(8,128)(2,1)}) custom-call(bf16[16,128,2048]{2,1,0:T(8,128)(2,1)} %select_select_fusion.refs_0_, bf16[1,2048]{1,0:T(2,128)(2,1)} %reshape.239.refs_1_), custom_call_target="tpu_custom_call" | custom-call | tf_op jit(solution)/shard_map/scatter_rows/pallas_call | solution.py:363
  97.0 0.0 copy-start.6
  97.0 52.8 %gather_rows.1 = bf16[16,128,2048]{2,1,0:T(8,128)(2,1)} custom-call(bf16[128,2048]{1,0:T(8,128)(2,1)} %get-tuple-element.9.own_ref), custom_call_target="tpu_custom_call" | custom-call | tf_op jit(solution)/shard_map/gather_rows/pallas_call | solution.py:413
  149.8 0.0 slice-start
  149.8 0.0 copy-start.2
  149.8 6.7 %convolution_convert_fusion.1 = bf16[2048,128]{1,0:T(8,128)(2,1)} fusion(bf16[2048,2048]{1,0:T(8,128)(2,1)} %bitcast.54, bf16[2048,128]{1,0:T(8,128)(2,1)} %param.21), kind=kOutput, calls=%fused_computation.12 | convolution fusion | flops 1074003968 | bytes 9437184 | tf_op jit(solution)/shard_map/bsd,dq->bsq/dot_general | solution.py:593
  156.6 0.0 slice-start.1
  156.6 0.0 copy-start.7
  156.6 6.5 %multiply_reduce_fusion = (f32[2048]{0:T(1024)S(1)}, f32[2048,128]{0,1:T(8,128)S(1)}) fusion(bf16[2048,2048]{1,0:T(8,128)(2,1)} %bitcast.55, bf16[2048,128]{1,0:T(8,128)(2,1)} %param.20), kind=kOutput, calls=%fused_computation.17 | convolution fusion | flops 1074264064 | bytes 9969664 | tf_op jit(solution)/shard_map/bsd,dq->bsq/dot_general | solution.py:590
  163.1 0.0 copy-done.6
  163.1 0.0 slice-done
  163.1 0.0 copy-done.2
  163.1 0.0 slice-done.1
  163.1 2.9 multiply_reduce_fusion.1
  166.0 0.6 maximum_bitcast_fusion.x_ref
  166.7 9.8 %group_sum.1 = f32[2,2048]{1,0:T(2,128)} custom-call(f32[2,2048]{1,0:T(2,128)} %maximum_bitcast_fusion.x_ref), custom_call_target="tpu_custom_call" | custom-call | tf_op jit(solution)/shard_map/group_sum/pallas_call | solution.py:444
  176.5 0.7 add_rsqrt_fusion
  177.2 0.0 copy-done.7
  177.2 0.3 multiply_bitcast_fusion
  177.5 2.5 fusion.17
  180.0 0.0 copy-start.8
  180.0 2.4 fusion.1
  182.4 0.0 copy-start.1
  182.4 5.7 %copy-done.1 = f32[2048,2048]{0,1:T(8,128)} copy-done((f32[2048,2048]{0,1:T(8,128)}, f32[2048,2048]{0,1:T(8,128)S(1)}, u32[]{:S(2)}) %copy-start.1) | copy-done | bytes 16777240
  188.1 4.7 fusion
  192.8 0.0 copy-done
  192.8 0.0 copy-done.8
  192.8 0.0 copy-start.5
  192.8 0.0 copy-start.3
  192.8 12.9 %convolution_convert_fusion = bf16[2048,2048]{1,0:T(8,128)(2,1)} fusion(bf16[128,2048]{1,0:T(8,128)(2,1)S(1)} %copy-done, bf16[2048,128]{1,0:T(8,128)(2,1)S(1)} %copy-done.8, f32[2048,2048]{0,1:T(8,128)} %copy-done.1, f32[2048]{0:T(1024)S(1)} %fusion, f32[2048]{0:T(1024)S(1)} %get-tuple-element.28), kind=kOutput, calls=%fused_computation.9 | convolution fusion | flops 2177105920 | bytes 26230784 | tf_op jit(solution)/shard_map/bqhd,hde->bqe/dot_general | solution.py:605
  205.7 0.0 copy-done.5
  205.8 0.6 reshape.245.refs_1_
  206.4 65.4 %scatter_rows.3 = (bf16[128,2048]{1,0:T(8,128)(2,1)}, bf16[128,2048]{1,0:T(8,128)(2,1)}) custom-call(bf16[16,128,2048]{2,1,0:T(8,128)(2,1)} %bitcast.63, bf16[1,2048]{1,0:T(2,128)(2,1)} %reshape.245.refs_1_, bf16[128,2048]{1,0:T(8,128)(2,1)} %get-tuple-element.10.refs_2_), custom_call_target="tpu_custom_call" | custom-call | tf_op jit(solution)/shard_map/scatter_rows/pallas_call | solution.py:363
  271.8 0.0 copy-done.3
  271.8 0.7 fusion.3
  272.5 0.3 copy.19
  272.9 1.1 copy.20
  273.9 244.4 %moe_layer.1 = bf16[128,2048]{1,0:T(8,128)(2,1)} custom-call(bf16[128,2048]{1,0:T(8,128)(2,1)} %get-tuple-element.11.own_ref, bf16[128,2048]{1,0:T(8,128)(2,1)} %get-tuple-element.12.hid_ref, f32[4,512,64]{2,1,0:T(8,128)} %bitcast.64, bf16[64,2048]{1,0:T(8,128)(2,1)} %bitcast.67, bf16[4096,2048]{1,0:T(8,128)(2,1)} %bitcast.60, bf16[4096,2048]{1,0:T(8,128)(2,1)} %bitcast.61, ...), custom_call_target="tpu_custom_call" | custom-call | tf_op jit(solution)/shard_map/moe_layer/pallas_call | solution.py:549
  518.3 1.9 copy.22
  (7 shorter events, 0.1 us)
Async XLA Ops:
  0.0 192.8 %copy-start = (bf16[128,2048]{1,0:T(8,128)(2,1)S(1)}, bf16[128,2048]{1,0:T(8,128)(2,1)}, u32[]{:S(2)}) copy-start(bf16[128,2048]{1,0:T(8,128)(2,1)} %param.22) | copy-start | bytes 1572868
  23.5 7.4 %copy-start.4 = (bf16[2048]{0:T(1024)(128)(2,1)S(1)}, bf16[2048]{0:T(1024)(128)(2,1)}, u32[]{:S(2)}) copy-start(bf16[2048]{0:T(1024)(128)(2,1)} %param.18) | copy-start | bytes 12292
  97.0 66.1 %copy-start.6 = (bf16[128]{0:T(256)(128)(2,1)S(1)}, bf16[128]{0:T(256)(128)(2,1)}, u32[]{:S(2)}) copy-start(bf16[128]{0:T(256)(128)(2,1)} %param.24) | copy-start | bytes 772
  149.8 13.3 %slice-start = ((s8[8388608]{0:T(1024)(128)(4,1)}), s8[4194304]{0:T(1024)(128)(4,1)S(1)}, s32[]{:S(2)}) async-start(s8[8388608]{0:T(1024)(128)(4,1)} %bitcast.56), calls=%async_computation | async-start | bytes 8388608
  149.8 13.3 %copy-start.2 = (bf16[2048,128]{1,0:T(8,128)(2,1)S(1)}, bf16[2048,128]{1,0:T(8,128)(2,1)}, u32[]{:S(2)}) copy-start(bf16[2048,128]{1,0:T(8,128)(2,1)} %param.19) | copy-start | bytes 1572868
  156.6 6.6 %slice-start.1 = ((s8[8388608]{0:T(1024)(128)(4,1)}), s8[4194304]{0:T(1024)(128)(4,1)S(1)}, s32[]{:S(2)}) async-start(s8[8388608]{0:T(1024)(128)(4,1)} %bitcast.56), calls=%async_computation.1 | async-start | bytes 8388608
  156.6 20.7 %copy-start.7 = (bf16[128]{0:T(256)(128)(2,1)S(1)}, bf16[128]{0:T(256)(128)(2,1)}, u32[]{:S(2)}) copy-start(bf16[128]{0:T(256)(128)(2,1)} %param.23) | copy-start | bytes 772
  180.0 12.8 %copy-start.8 = (bf16[2048,128]{1,0:T(8,128)(2,1)S(1)}, bf16[2048,128]{1,0:T(8,128)(2,1)}, u32[]{:S(2)}) copy-start(bf16[2048,128]{1,0:T(8,128)(2,1)} %convolution_convert_fusion.1) | copy-start | bytes 1572868
  182.4 5.7 %copy-start.1 = (f32[2048,2048]{0,1:T(8,128)}, f32[2048,2048]{0,1:T(8,128)S(1)}, u32[]{:S(2)}) copy-start(f32[2048,2048]{0,1:T(8,128)S(1)} %get-tuple-element.29) | copy-start | bytes 50331652
  192.8 12.9 %copy-start.5 = (bf16[2048]{0:T(1024)(128)(2,1)S(1)}, bf16[2048]{0:T(1024)(128)(2,1)}, u32[]{:S(2)}) copy-start(bf16[2048]{0:T(1024)(128)(2,1)} %param.25) | copy-start | bytes 12292
  192.8 79.0 %copy-start.3 = (s32[1,2048,8]{1,2,0:T(8,128)S(1)}, s32[1,2048,8]{1,2,0:T(8,128)}, u32[]{:S(2)}) copy-start(s32[1,2048,8]{1,2,0:T(8,128)} %param.16) | copy-start | bytes 196612
